TPU v7x, 128 devices: a whole 4x4x4 slice. The times are simulated.
128 devices in a mesh: grp: 4 (over y_hi, core), row: 32 (over y_lo, z, x).
Axes of the slice: x: 4, y: 4 (y_hi: 2, y_lo: 2; y = y_hi * 2 + y_lo), z: 4, core: 2. Of those that a mesh axis runs over, the one named last changes fastest.
Arguments:
- landmarks: bfloat16 [4096, 1024], P(('grp', 'row')), may hold values from -6.5 to 6.5
- initial_basis: bfloat16 [4096, 256], P(('grp', 'row')), may hold values from -0.09375 to 0.09375
- points: bfloat16 [131072, 1024], P(('grp', 'row')), may hold values from -6.5 to 6.5
Outputs:
- basis: float32 [4096, 256], P(('grp', 'row'))
- coords: float32 [131072, 256], P(('grp', 'row'))
All inputs are finite; a program needn't handle non-finite values.
Results may differ from a plain program's by a relative error of at most 0.0057.
Values may be sent and summed in bfloat16 or wider, within the bound.
A program may use at most 128 MiB of HBM per device.

v0:
```python
import math

import jax
import jax.numpy as jnp
from jax import lax
from jax.sharding import PartitionSpec as P

ITERS = 2


spread = 0.25


def laid_out(blocks, dim):
    blocks = jnp.moveaxis(blocks, 0, dim)
    shape = blocks.shape
    return blocks.reshape(*shape[:dim], shape[dim] * shape[dim + 1], *shape[dim + 2 :])


def copy_for_each(x, axis):
    devices = lax.axis_size(axis)
    return lax.all_to_all(jnp.broadcast_to(x[None], (devices, *x.shape)), axis, 0, 0, tiled=True)


def collect(x, axis, dim):
    return laid_out(copy_for_each(x, axis), dim)


def of_everyone(x, axis):
    return copy_for_each(x, axis).sum(axis=0)


def in_blocks(x, dim, devices):
    shape = x.shape
    blocks = x.reshape(*shape[:dim], devices, shape[dim] // devices, *shape[dim + 1 :])
    return jnp.moveaxis(blocks, dim, 0)


def sum_at_owner(x, axis, dim):
    devices = lax.axis_size(axis)
    blocks = lax.all_to_all(in_blocks(x, dim, devices), axis, 0, 0, tiled=True)
    return jnp.sum(blocks, axis=0)


def side_by_side(arrays, axis, dim, along):
    columns = [a.reshape(*a.shape[:along], -1) for a in arrays]
    both = jnp.concatenate(columns, axis=along)
    out, at, gathered = (lax.psum_scatter(both, axis, scatter_dimension=dim, tiled=True), 0, [])
    for a, column in zip(arrays, columns):
        share = out[..., at : at + column.shape[along]]
        gathered.append(share.reshape(*share.shape[:along], *a.shape[along:]))
        at += column.shape[along]
    return tuple(gathered)


def squared_rows(rows):
    return jnp.sum(jnp.square(rows.astype(jnp.float32)), axis=1)


def pair_kernel(left, right):
    inner = lax.dot_general(
        left, right, (((1,), (1,)), ((), ())), preferred_element_type=jnp.float32
    )
    dist = squared_rows(left)[:, None] + squared_rows(right)[None, :] - 2.0 * inner
    return jnp.exp(-dist / (spread * left.shape[1]))


def point_terms(anchors, spectral_rows, members, member_sq):
    inner = lax.dot_general(
        anchors, members, (((1,), (1,)), ((), ())), preferred_element_type=jnp.float32
    )
    dist = squared_rows(anchors)[:, None] + member_sq[None, :] - 2.0 * inner
    kernel_part = jnp.exp(-dist / (spread * anchors.shape[1]))
    degree_part = jnp.sum(kernel_part, axis=0)
    numer_part = lax.dot_general(
        kernel_part.astype(jnp.bfloat16),
        spectral_rows,
        (((0,), (0,)), ((), ())),
        preferred_element_type=jnp.float32,
    )
    return (numer_part, degree_part)


def body(landmarks, initial_basis, points):
    local_rows = landmarks.shape[0]
    total = local_rows * lax.axis_size("grp") * lax.axis_size("row")
    row_index = lax.axis_index("row")
    group_rows = lax.all_gather(landmarks, "row", axis=0, tiled=True)
    cross_rows = collect(landmarks, "grp", 0)
    land_kernel = pair_kernel(group_rows, cross_rows)
    group_degree = of_everyone(jnp.sum(land_kernel, axis=1), "row")
    own_degree = lax.dynamic_slice_in_dim(group_degree, row_index * local_rows, local_rows, 0)
    cross_degree = collect(own_degree, "grp", 0)
    row_scale = 1.0 / jnp.sqrt(group_degree)
    column_scale = 1.0 / jnp.sqrt(cross_degree)
    affinity = (land_kernel * row_scale[:, None] * column_scale[None, :]).astype(jnp.bfloat16)
    current = initial_basis
    for step in range(ITERS):
        cross_basis = collect(current, "grp", 0)
        image = sum_at_owner(
            jnp.dot(affinity, cross_basis, preferred_element_type=jnp.float32), "row", 0
        )
        gram = lax.psum(jnp.dot(image.T, image, precision=lax.Precision.HIGHEST), ("grp", "row"))
        lower = jnp.linalg.cholesky(gram)
        ortho = jax.scipy.linalg.solve_triangular(lower, image.T, lower=True).T
        current = ortho.astype(jnp.bfloat16)
    lam = jnp.diagonal(lower)
    own_scale = 1.0 / jnp.sqrt(own_degree)
    spectral = (ortho * own_scale[:, None] / lam[None, :]).astype(jnp.bfloat16)
    group_spectral = collect(spectral, "row", 0)
    cross_points = lax.all_gather(points, "grp", axis=0, tiled=True)
    numer_part, degree_part = point_terms(
        group_rows, group_spectral, cross_points, squared_rows(cross_points)
    )
    numer, degree = side_by_side((numer_part, degree_part), "grp", 0, 1)
    coords = numer / jnp.sqrt(degree)[:, None] * math.sqrt(total)
    return (ortho, coords)


def solution(mesh):
    in_specs = (P(("grp", "row"), None), P(("grp", "row"), None), P(("grp", "row"), None))
    out_specs = (P(("grp", "row"), None), P(("grp", "row"), None))
    return jax.shard_map(body, mesh=mesh, in_specs=in_specs, out_specs=out_specs, check_vma=False)
```

profile of v0, /device:TPU:1, one launch (start us, length us, event | category | flops | bytes accessed | tf_op | source)
XLA Modules:
  0.0 810.4 jit_solution(4297087186044760652)
XLA Ops:
  9.6 12.2 %all_to_all.42 = bf16[4,32,1024]{2,1,0:T(8,128)(2,1)S(1)} all-to-all(bf16[4,32,1024]{2,1,0:T(8,128)(2,1)S(1)} %broadcast_in_dim.14), channel_id=1, replica_groups=mesh['grp'=4,'row'=32] {'grp'}, dimensions={0} | all-to-all | bytes 524288 | tf_op jit(solution)/shard_map/all_to_all | solution.py:22
  22.0 122.9 %all-gather.3.cloned.1.call-done = bf16[1024,1024]{1,0:T(8,128)(2,1)} async-done(((bf16[32,1024]{1,0:T(8,128)(2,1)}), bf16[1024,1024]{1,0:T(8,128)(2,1)}) %all-gather.3.cloned.1.call-update) | async-done | bytes 2097168 | tf_op jit(solution)/shard_map/all_gather | solution.py:88
  150.2 6.2 all-to-all-start.1
  156.4 7.3 all-to-all-done.1
  164.5 28.1 %all-to-all-start.2 = ((f32[4,1,32]{2,1,0:T(1,128)}), f32[4,1,32]{2,1,0:T(1,128)S(1)}, u32[]{:S(2)}, u32[]{:S(2)}) async-start(f32[4,1,32]{2,1,0:T(1,128)} %broadcast_in_dim.16), calls=%async_computation.2 | async-start | bytes 4096 | tf_op jit(solution)/shard_map/all_to_all | solution.py:22
  192.6 4.5 all-to-all-done.2
  207.4 19.0 %all_to_all.44 = f32[32,32,256]{2,1,0:T(8,128)S(1)} all-to-all(f32[32,32,256]{2,1,0:T(8,128)S(1)} %fusion.39), channel_id=1, replica_groups=mesh['grp'=4,'row'=32] {'row'}, dimensions={0} | all-to-all | bytes 2097152 | tf_op jit(solution)/shard_map/all_to_all | solution.py:41
  227.9 140.6 %all-reduce.4.cloned.1.call-done = f32[256,256]{0,1:T(8,128)} async-done(((f32[256,256]{0,1:T(8,128)}), f32[256,256]{0,1:T(8,128)}) %all-reduce.4.cloned.1.call-update) | async-done | bytes 262160 | tf_op jit(solution)/shard_map/psum | solution.py:103
  370.6 11.7 %cholesky.130 = f32[128,128]{1,0:T(8,128)S(1)} custom-call(f32[128,128]{1,0:T(8,128)S(1)} %cholesky.194), custom_call_target="Cholesky" | custom-call | tf_op jit(solution)/shard_map/jit(cholesky)/cholesky | solution.py:104
  382.4 9.8 %custom-call.15 = f32[1,128,128]{1,2,0:T(8,128)S(1)} custom-call(f32[1,128,128]{2,1,0:T(8,128)S(1)} %get-tuple-element.63), custom_call_target="InvertDiagBlocksLowerTriangular" | custom-call | tf_op jit(solution)/shard_map/jit(cholesky)/cholesky | solution.py:104
  392.7 11.7 %cholesky.147 = f32[128,128]{1,0:T(8,128)S(1)} custom-call(f32[128,128]{1,0:T(8,128)S(1)} %convolution_subtract_fusion.1), custom_call_target="Cholesky" | custom-call | tf_op jit(solution)/shard_map/jit(cholesky)/cholesky | solution.py:104
  410.8 19.7 %custom-call.16 = f32[2,128,128]{1,2,0:T(8,128)S(1)} custom-call(f32[2,128,128]{2,1,0:T(8,128)S(1)} %get-tuple-element.18), custom_call_target="InvertDiagBlocksLowerTriangular" | custom-call | tf_op jit(solution)/shard_map/jit(_solve_triangular)/triangular_solve | solution.py:105
  431.1 8.7 %all_to_all.43 = bf16[4,32,256]{2,1,0:T(8,128)(2,1)S(1)} all-to-all(bf16[4,32,256]{2,1,0:T(8,128)(2,1)S(1)} %broadcast_in_dim.18), channel_id=1, replica_groups=mesh['grp'=4,'row'=32] {'grp'}, dimensions={0} | all-to-all | bytes 131072 | tf_op jit(solution)/shard_map/all_to_all | solution.py:22
  440.1 19.6 %all_to_all.45 = f32[32,32,256]{2,1,0:T(8,128)S(1)} all-to-all(f32[32,32,256]{2,1,0:T(8,128)S(1)} %fusion.41), channel_id=1, replica_groups=mesh['grp'=4,'row'=32] {'row'}, dimensions={0} | all-to-all | bytes 2097152 | tf_op jit(solution)/shard_map/all_to_all | solution.py:41
  461.5 183.0 %all-reduce.6.cloned.1.call-done = f32[256,256]{0,1:T(8,128)} async-done(((f32[256,256]{0,1:T(8,128)}), f32[256,256]{0,1:T(8,128)}) %all-reduce.6.cloned.1.call-update) | async-done | bytes 262160 | tf_op jit(solution)/shard_map/psum | solution.py:103
  646.7 11.7 %cholesky.164 = f32[128,128]{1,0:T(8,128)S(1)} custom-call(f32[128,128]{1,0:T(8,128)S(1)} %cholesky.197), custom_call_target="Cholesky" | custom-call | tf_op jit(solution)/shard_map/jit(cholesky)/cholesky | solution.py:104
  658.4 9.8 %custom-call.17 = f32[1,128,128]{1,2,0:T(8,128)S(1)} custom-call(f32[1,128,128]{2,1,0:T(8,128)S(1)} %get-tuple-element.59), custom_call_target="InvertDiagBlocksLowerTriangular" | custom-call | tf_op jit(solution)/shard_map/jit(cholesky)/cholesky | solution.py:104
  668.7 11.7 %cholesky.181 = f32[128,128]{1,0:T(8,128)S(1)} custom-call(f32[128,128]{1,0:T(8,128)S(1)} %convolution_subtract_fusion), custom_call_target="Cholesky" | custom-call | tf_op jit(solution)/shard_map/jit(cholesky)/cholesky | solution.py:104
  687.4 19.7 %custom-call.18 = f32[2,128,128]{1,2,0:T(8,128)S(1)} custom-call(f32[2,128,128]{2,1,0:T(8,128)S(1)} %get-tuple-element.19), custom_call_target="InvertDiagBlocksLowerTriangular" | custom-call | tf_op jit(solution)/shard_map/jit(_solve_triangular)/triangular_solve | solution.py:105
  711.5 5.0 all-to-all-start.7
  716.5 5.2 multiply_reduce_fusion
  722.3 13.9 %fusion = (f32[4096]{0:T(1024)S(1)}, f32[1024,4096]{1,0:T(8,128)}) fusion(f32[4096]{0:T(1024)S(1)} %multiply_reduce_fusion, f32[1024]{0:T(1024)S(1)} %multiply_reduce_fusion.1, bf16[1024,1024]{1,0:T(8,128)(2,1)S(1)} %copy-done.1, bf16[4096,1024]{1,0:T(8,128)(2,1)S(1)} %copy-done), kind=kOutput, calls=%fused_computation.7 | convolution fusion | flops 8615096320 | bytes 27299840 | tf_op jit(solution)/shard_map/dot_general | solution.py:69
  736.2 8.2 %fusion.2 = f32[4096,256]{0,1:T(8,128)S(1)} fusion(bf16[1024,256]{1,0:T(8,128)(2,1)S(1)} %bitcast.102, f32[1024,4096]{1,0:T(8,128)} %get-tuple-element.71, f32[4096]{0:T(1024)S(1)} %multiply_reduce_fusion, f32[1024]{0:T(1024)S(1)} %multiply_reduce_fusion.1), kind=kOutput, calls=%fused_computation.9 | convolution fusion | flops 2172649472 | bytes 21516288 | tf_op jit(solution)/shard_map/dot_general | solution.py:75
  746.7 52.7 %reduce-scatter.2.cloned.1.call-done = f32[1024,257]{0,1:T(8,128)} async-done(((f32[4096,257]{0,1:T(8,128)}), f32[1024,257]{0,1:T(8,128)}) %reduce-scatter.2.cloned.1.call-update) | async-done | bytes 1052688 | tf_op jit(solution)/shard_map/reduce_scatter | solution.py:48
  (93 shorter events, 56.7 us)
Async XLA Ops:
  8.0 137.0 %all-gather.3.cloned.1.call-start = ((), (), s32[]{:S(2)}) async-start(), calls=%async_computation.9 | async-start | bytes 2162688 | tf_op jit(solution)/shard_map/all_gather | solution.py:88
  150.2 13.5 %all-to-all-start.1 = ((f32[32,1,1024]{2,1,0:T(1,128)}), f32[32,1,1024]{2,1,0:T(1,128)S(1)}, u32[]{:S(2)}, u32[]{:S(2)}) async-start(f32[32,1,1024]{2,1,0:T(1,128)} %broadcast_in_dim.15), calls=%async_computation.1 | async-start | bytes 262144 | tf_op jit(solution)/shard_map/all_to_all | solution.py:22
  164.5 32.6 %all-to-all-start.2 = ((f32[4,1,32]{2,1,0:T(1,128)}), f32[4,1,32]{2,1,0:T(1,128)S(1)}, u32[]{:S(2)}, u32[]{:S(2)}) async-start(f32[4,1,32]{2,1,0:T(1,128)} %broadcast_in_dim.16), calls=%async_computation.2 | async-start | bytes 4096 | tf_op jit(solution)/shard_map/all_to_all | solution.py:22
  198.4 8.7 %all-to-all-start.3 = ((bf16[4,32,256]{2,1,0:T(8,128)(2,1)}), bf16[4,32,256]{2,1,0:T(8,128)(2,1)S(1)}, u32[]{:S(2)}, u32[]{:S(2)}) async-start(bf16[4,32,256]{2,1,0:T(8,128)(2,1)} %broadcast_in_dim.17), calls=%async_computation.3 | async-start | bytes 131072 | tf_op jit(solution)/shard_map/all_to_all | solution.py:22
  202.4 166.1 %all-reduce.4.cloned.1.call-start = ((), (), s32[]{:S(2)}) async-start(), calls=%async_computation.10 | async-start | bytes 524288 | tf_op jit(solution)/shard_map/psum | solution.py:103
  227.7 416.9 %all-reduce.6.cloned.1.call-start = ((), (), s32[]{:S(2)}) async-start(), calls=%async_computation.11 | async-start | bytes 524288 | tf_op jit(solution)/shard_map/psum | solution.py:103
  460.9 255.6 %all-gather.5.cloned.1.call-start = ((), (), s32[]{:S(2)}) async-start(), calls=%async_computation.12 | async-start | bytes 10485760 | tf_op jit(solution)/shard_map/all_gather | solution.py:111
  461.5 260.3 %copy-start.1 = (bf16[1024,1024]{1,0:T(8,128)(2,1)S(1)}, bf16[1024,1024]{1,0:T(8,128)(2,1)}, u32[]{:S(2)}) copy-start(bf16[1024,1024]{1,0:T(8,128)(2,1)} %all-gather.3.cloned.1.call-done) | copy-start | bytes 6291460
  711.5 24.7 %all-to-all-start.7 = ((bf16[32,32,256]{2,1,0:T(8,128)(2,1)}), bf16[32,32,256]{2,1,0:T(8,128)(2,1)S(1)}, u32[]{:S(2)}, u32[]{:S(2)}) async-start(bf16[32,32,256]{2,1,0:T(8,128)(2,1)} %broadcast_in_dim.19), calls=%async_computation.7 | async-start | bytes 1048576 | tf_op jit(solution)/shard_map/all_to_all | solution.py:22
  716.4 83.0 %reduce-scatter.2.cloned.1.call-start = ((), (), s32[]{:S(2)}) async-start(), calls=%async_computation.13 | async-start | bytes 5406720 | tf_op jit(solution)/shard_map/reduce_scatter | solution.py:48
  716.5 5.8 copy-start
Sparse Core Ops, SparseCore 0:
  10.4 134.4 all-gather.2
  227.8 140.6 all-reduce.3
  461.1 183.4 all-reduce.5
Sparse Core Ops, SparseCore 1:
  463.1 60.4 all-gather.4
  746.8 52.6 reduce-scatter.1
where the time goes:
time: 815 us; the launch traced here: 810 us
  waiting for transfers between devices  517 us (63%)
  other arithmetic  122 us (15%)
  blocking collectives  59.6 us (7%)
  starting transfers between devices  43.6 us (5%)
  matrix products  29.3 us (4%)
  local copies, waits for them, and re-layouts  19.8 us (2%)
  between operations  18.6 us (2%)
    psum x2, waiting for transfers between devices, body(): lax.psum(jnp.dot(image.T, image, precision=lax.Precision.HIGHEST), ('grp'...  324 us
    all_gather x1, waiting for transfers between devices, body(): group_rows = lax.all_gather(landmarks, 'row', axis=0, tiled=True)  123 us
    another operation x13, other arithmetic, body(): lower = jnp.linalg.cholesky(gram)  68.6 us
    reduce_scatter x1, waiting for transfers between devices, side_by_side(): lax.psum_scatter(both, axis, scatter_dimension=dim, tiled=True)  52.7 us
    all_to_all x4, starting transfers between devices, copy_for_each(): lax.all_to_all(jnp.broadcast_to(x[None], (devices, *x.shape)), axis, 0, 0...  43.2 us
    another operation x5, other arithmetic, body(): ortho = jax.scipy.linalg.solve_triangular(lower, image.T, lower=True).T  39.4 us
    all_to_all x2, blocking collectives, sum_at_owner(): blocks = lax.all_to_all(in_blocks(x, dim, devices), axis, 0, 0, tiled=True)  38.7 us
    all_to_all x2, blocking collectives, copy_for_each(): lax.all_to_all(jnp.broadcast_to(x[None], (devices, *x.shape)), axis, 0, 0...  20.9 us
  transfers between devices with their start and end apart: 9, of which 7 were waited for; matrix products, arithmetic and copies ran while one was open for 11% of the time, Pallas kernels for 0%

commit v1 on v0

v1 whole, which is shorter than its diff:
```python
import functools
import math

import jax
import jax.numpy as jnp
from jax import lax
from jax.experimental import pallas as pl
from jax.experimental.pallas import tpu as pltpu
from jax.sharding import PartitionSpec as P

ITERS = 2
SPREAD = 0.25
LOG2E = 1.4426950408889634
MESH = pl.DeviceIdType.MESH
F32 = jnp.float32
BF16 = jnp.bfloat16
VMEM_LIMIT = 67_043_328


def place():
    grp, row = lax.axis_index("grp"), lax.axis_index("row")
    core, y_hi = lax.rem(grp, 2), grp // 2
    y_lo, z, x = row // 16, lax.rem(row // 4, 4), lax.rem(row, 4)
    return core, {"z": z, "y": y_hi * 2 + y_lo, "x": x}


def device(core, at):
    return ((at["y"] // 2) * 2 + core, lax.rem(at["y"], 2) * 16 + at["z"] * 4 + at["x"])


def neighbour(core, at, axis, by):
    return device(core, {**at, axis: lax.rem(at[axis] + by + 4, 4)})


def dot_nt(a, b):
    return lax.dot_general(a, b, (((1,), (1,)), ((), ())), preferred_element_type=F32)


def dot_tn(a, b):
    return lax.dot_general(a, b, (((0,), (0,)), ((), ())), preferred_element_type=F32)


ORDERS = (("x", "y", "z"), ("y", "z", "x"), ("z", "x", "y"))


def gather_kernel(
    scale, land_in, basis_in, points_ref,
    weights_out, factor_ref, land_out, basis_out, sq_out,
    land, basis, sq, wbuf, dacc,
    own_sem, send_sem, recv_sem, fsend, frecv, out_sem, w_sem,
):
    core, at = place()
    partner = device(1 - core, at)
    own = (core, at["z"], at["y"], at["x"])
    first = [
        pltpu.make_async_copy(land_in, land.at[own], own_sem.at[0]),
        pltpu.make_async_copy(basis_in, basis.at[own], own_sem.at[1]),
    ]
    for c in first:
        c.start()

    barrier = pltpu.get_barrier_semaphore()
    peers = [neighbour(core, at, a, by) for a in "xyz" for by in (1, -1)] + [partner]
    for peer in peers:
        pl.semaphore_signal(barrier, inc=1, device_id=peer, device_id_type=MESH)
    for c in first:
        c.wait()
    pl.semaphore_wait(barrier, len(peers))

    parts = (
        (land, pl.ds(0, 384), ORDERS[0]),
        (land, pl.ds(384, 384), ORDERS[1]),
        (land, pl.ds(768, 256), ORDERS[2]),
        (basis, pl.ds(0, 256), ORDERS[2]),
    )

    def block(part, phase, shift, rows=slice(None)):
        buf, cols, order = part
        index = [core]
        for a in "zyx":
            if a == order[phase]:
                index.append(lax.rem(at[a] + shift + 4, 4))
            elif a in order[:phase]:
                index.append(slice(None))
            else:
                index.append(at[a])
        return buf.at[tuple(index + [rows, cols])]

    def remote(ref, sems, index, dev):
        return pltpu.make_async_remote_copy(
            src_ref=ref, dst_ref=ref, send_sem=sems[0].at[index], recv_sem=sems[1].at[index],
            device_id=dev, device_id_type=MESH,
        )

    sent, forwarded = [], []

    def send(ref, index, dev):
        c = remote(ref, (send_sem, recv_sem), index, dev)
        c.start()
        sent.append(c)
        return c

    def forward(ref, index):
        c = remote(ref, (fsend, frecv), index, partner)
        c.start()
        forwarded.append(c)

    np_ = len(parts)
    for p, part in enumerate(parts):
        forward(block(part, 0, 0), p * 10)
    for phase in range(3):
        ring = []
        for p, part in enumerate(parts):
            a = part[2][phase]
            base = (p * 3 + phase) * 4
            up, down = neighbour(core, at, a, 1), neighbour(core, at, a, -1)
            mine = block(part, phase, 0)
            ring.append((send(mine, base, up), send(mine, base + 1, down), up, down, base))
        second = []
        for p, part in enumerate(parts):
            from_below, from_above, up, down, base = ring[p]
            from_below.wait_recv()
            far_up = send(block(part, phase, -1, pl.ds(0, 16)), base + 2, up)
            from_above.wait_recv()
            far_down = send(block(part, phase, 1, pl.ds(16, 16)), base + 3, down)
            forward(block(part, phase, -1), p * 10 + 1 + phase * 3)
            forward(block(part, phase, 1), p * 10 + 2 + phase * 3)
            second.append((far_up, far_down))
        for p, part in enumerate(parts):
            far_up, far_down = second[p]
            far_up.wait_recv()
            far_down.wait_recv()
            forward(block(part, phase, 2), p * 10 + 3 + phase * 3)
    for c in forwarded:
        c.wait_recv()

    outs = [
        pltpu.make_async_copy(land, land_out, out_sem.at[0]),
        pltpu.make_async_copy(basis, basis_out, out_sem.at[1]),
    ]
    for c in outs:
        c.start()

    def norms(b, _):
        c, z, y = b // 16, lax.rem(b // 4, 4), lax.rem(b, 4)
        rows = land[c, z, y].reshape(128, 1024).astype(F32)
        squares = rows * rows
        part = squares[:, :128]
        for k in range(1, 8):
            part += squares[:, k * 128 : (k + 1) * 128]
        line = jnp.sum(part.T, axis=0, keepdims=True) * scale
        sq[:, pl.ds(pl.multiple_of(b * 128, 128), 128)] = line
        return 0

    lax.fori_loop(0, 32, norms, 0)
    sq_copy = pltpu.make_async_copy(sq, sq_out, out_sem.at[2])
    sq_copy.start()

    tile = 256
    tiles = points_ref.shape[0] // tile
    copies = []
    for t in range(tiles):
        slot = t % 2
        if t >= 2:
            copies[t - 2].wait()
        pts = points_ref[pl.ds(t * tile, tile), :]
        wide = pts.astype(F32)
        psq = jnp.sum(wide * wide, axis=1, keepdims=True) * scale
        dacc[...] = jnp.zeros_like(dacc)

        def chunk(j, _):
            c, z = j // 4, lax.rem(j, 4)
            rows = land[c, z].reshape(512, 1024)
            cols = pl.ds(pl.multiple_of(j * 512, 512), 512)
            near = jnp.exp2(dot_nt(pts, rows) * (2.0 * scale) - (psq + sq[:, cols]))
            wbuf[slot, :, cols] = near.astype(BF16)
            dacc[...] += near[:, :128] + near[:, 128:256] + near[:, 256:384] + near[:, 384:]
            return 0

        lax.fori_loop(0, 8, chunk, 0)
        factor_ref[pl.ds(t * tile, tile), :] = 64.0 / jnp.sqrt(jnp.sum(dacc[...], axis=1, keepdims=True))
        copies.append(
            pltpu.make_async_copy(wbuf.at[slot], weights_out.at[pl.ds(t * tile, tile), :], w_sem.at[slot])
        )
        copies[-1].start()
    for c in copies[-2:]:
        c.wait()
    for c in sent:
        c.wait_send()
    for c in forwarded:
        c.wait_send()
    for c in outs:
        c.wait()
    sq_copy.wait()


def split(x):
    hi = x.astype(BF16)
    return hi, (x - hi.astype(F32)).astype(BF16)


def cholesky_inverse(aug, lower_t, inverse):
    lane = 128
    row_id = lax.broadcasted_iota(jnp.int32, (16, lane), 0)
    for b in range(16):
        r0 = b * 16
        diag = aug[pl.ds(r0, 16), :256]
        reps = [jnp.broadcast_to(diag[:, r0 + j : r0 + j + 1], (16, lane)) for j in range(16)]
        panel = [aug[pl.ds(r0, 16), pl.ds(k * lane, lane)] for k in range(4)]
        for j in range(16):
            root = lax.rsqrt(reps[j][j : j + 1, :])
            column = reps[j] * root
            for i in range(j + 1, 16):
                reps[i] = reps[i] - column * column[i : i + 1, :]
            below = jnp.where(row_id > j, column, 0.0)
            for k in range(4):
                line = panel[k][j : j + 1, :] * root
                panel[k] = jnp.where(row_id == j, line, panel[k] - below * line)
        for k in range(2):
            lower_t[pl.ds(r0, 16), pl.ds(k * lane, lane)] = panel[k]
            inverse[pl.ds(r0, 16), pl.ds(k * lane, lane)] = panel[2 + k]
        if b < 15:
            rows = jnp.concatenate(panel, axis=1)
            hi = rows.astype(BF16)
            rest = rows - hi.astype(F32)
            mid = rest.astype(BF16)
            low = (rest - mid.astype(F32)).astype(BF16)
            left = jnp.concatenate([hi, hi, mid, mid, hi, low], axis=0)[:, :256]
            right = jnp.concatenate([hi, mid, hi, mid, low, hi], axis=0)
            start = (r0 + 16) // 128 * 128
            aug[start:, :] = aug[start:, :] - dot_tn(left[:, start:], right)


def main_kernel(
    scale, land_hbm, basis_hbm, sq_ref,
    own_out, spectral_out,
    kern, xs, csum, grams, aug, lower_t, inverse, col_scale, row_scale, gacc, staged,
    in_sem, c_sem, g_sem, x_sem, s_sem, l_sem,
):
    core, at = place()
    other = 1 - core
    partner = device(other, at)
    half = kern.shape[0]
    tile, tiles = 256, half // 256
    mine = pl.multiple_of(core * half, half)

    def remote(src, dst, sems, index):
        return pltpu.make_async_remote_copy(
            src_ref=src, dst_ref=dst, send_sem=sems.at[0, index], recv_sem=sems.at[1, index],
            device_id=partner, device_id_type=MESH,
        )

    basis_in = pltpu.make_async_copy(basis_hbm, xs.at[0], in_sem.at[1])
    basis_in.start()
    barrier = pltpu.get_barrier_semaphore()
    pl.semaphore_signal(barrier, inc=1, device_id=partner, device_id_type=MESH)

    csum[0] = jnp.zeros(csum.shape[1:], F32)

    def kernel_scope(land):
        land_in = pltpu.make_async_copy(land_hbm, land, in_sem.at[0])
        land_in.start()
        land_in.wait()

        def row_tile(t, _):
            r = pl.ds(pl.multiple_of(t * tile, tile), tile)
            rows = land[pl.ds(pl.multiple_of(mine + t * tile, tile), tile), :]
            wide = rows.astype(F32)
            rsq = jnp.sum(wide * wide, axis=1, keepdims=True) * scale
            gacc[:, :128] = jnp.zeros((tile, 128), F32)

            def chunk(j, _):
                cols = pl.ds(pl.multiple_of(j * 512, 512), 512)
                near = jnp.exp2(dot_nt(rows, land[cols, :]) * (2.0 * scale) - (rsq + sq_ref[:, cols]))
                kern[r, cols] = near
                gacc[:, :128] += near[:, :128] + near[:, 128:256] + near[:, 256:384] + near[:, 384:]
                csum[0, :, cols] += jnp.sum(near.reshape(tile // 8, 8, 512), axis=0)
                return 0

            lax.fori_loop(0, 8, chunk, 0)
            col_scale[r, :] = 1.0 / jnp.sqrt(jnp.sum(gacc[:, :128], axis=1, keepdims=True))
            return 0

        lax.fori_loop(0, tiles, row_tile, 0)

    pl.run_scoped(kernel_scope, pltpu.VMEM(land_hbm.shape, BF16))
    pl.semaphore_wait(barrier, 1)
    give = remote(csum.at[0], csum.at[1], c_sem, 0)
    give.start()
    give.wait_recv()
    degree = jnp.sum(csum[0] + csum[1], axis=0, keepdims=True)
    row_scale[...] = 1.0 / jnp.sqrt(degree)
    give.wait_send()
    basis_in.wait()

    pending = []

    def iterate(affinity, image):
        eye = (
            lax.broadcasted_iota(jnp.int32, (256, 256), 0) == lax.broadcasted_iota(jnp.int32, (256, 256), 1)
        )
        for step in range(ITERS):
            gacc[...] = jnp.zeros_like(gacc)

            def image_tile(t, _):
                r = pl.ds(pl.multiple_of(t * tile, tile), tile)
                if step == 0:
                    scale_rows = col_scale[r, :]
                    for j in range(8):
                        cols = pl.ds(j * 512, 512)
                        affinity[r, cols] = (kern[r, cols] * scale_rows * row_scale[:, cols]).astype(BF16)
                img = jnp.dot(affinity[r, :], xs[step], preferred_element_type=F32)
                image[r, :] = img
                hi, lo = split(img)
                gacc[...] += dot_tn(hi, jnp.concatenate([hi, lo], axis=1))
                return 0

            lax.fori_loop(0, tiles, image_tile, 0)
            cross = gacc[:, 256:]
            grams[step, 0] = gacc[:, :256] + cross + cross.T
            swap = remote(grams.at[step, 0], grams.at[step, 1], g_sem, step)
            swap.start()
            swap.wait_recv()
            aug[:, :256] = grams[step, 0] + grams[step, 1]
            aug[:, 256:] = jnp.where(eye, 1.0, 0.0)
            swap.wait_send()
            cholesky_inverse(aug, lower_t, inverse)
            ihi, ilo = split(inverse[...])
            weights = jnp.concatenate([ihi, ilo, ihi], axis=1)
            last = step == ITERS - 1
            if last:
                lam = jnp.sum(jnp.where(eye, lower_t[...], 0.0), axis=0, keepdims=True)

            def ortho_tile(t, _):
                r = pl.ds(pl.multiple_of(t * tile, tile), tile)
                hi, lo = split(image[r, :])
                ortho = dot_nt(jnp.concatenate([hi, hi, lo], axis=1), weights)
                if last:
                    image[r, :] = ortho
                    staged[r, :] = (ortho * col_scale[r, :] / lam).astype(BF16)
                else:
                    xs[step + 1, pl.ds(pl.multiple_of(mine + t * tile, tile), tile), :] = ortho.astype(BF16)
                return 0

            lax.fori_loop(0, tiles, ortho_tile, 0)
            if last:
                give = remote(staged, spectral_out.at[pl.ds(mine, half), :], s_sem, 0)
                give.start()
                local = pltpu.make_async_copy(staged, spectral_out.at[pl.ds(mine, half), :], l_sem)
                local.start()
                index = at["z"] * 16 + at["y"] * 4 + at["x"]
                own_out[...] = image[pl.ds(pl.multiple_of(index * 32, 32), 32), :]
                local.wait()
                give.wait_recv()
                give.wait_send()
            else:
                part = xs.at[step + 1, pl.ds(mine, half), :]
                give = remote(part, part, x_sem, step)
                give.start()
                give.wait_recv()
                pending.append(give)
        for c in pending:
            c.wait_send()

    pl.run_scoped(iterate, pltpu.VMEM(kern.shape, BF16), pltpu.VMEM((half, 256), F32))


def coords_kernel(weights_ref, spectral_ref, factor_ref, out_ref):
    numer = jnp.dot(weights_ref[...], spectral_ref[...], preferred_element_type=F32)
    out_ref[...] = numer * factor_ref[...]


def body(landmarks, initial_basis, points):
    shard, width = landmarks.shape
    rank = initial_basis.shape[1]
    total = shard * 128
    half = total // 2
    count = points.shape[0]
    scale = LOG2E / (SPREAD * width)
    anywhere = pl.BlockSpec(memory_space=pl.ANY)
    vmem = pl.BlockSpec(memory_space=pltpu.VMEM)
    dma = pltpu.SemaphoreType.DMA

    weights, factor, land, basis, sq = pl.pallas_call(
        functools.partial(gather_kernel, scale),
        name="gather",
        out_shape=(
            jax.ShapeDtypeStruct((count, total), BF16),
            jax.ShapeDtypeStruct((count, 1), F32),
            jax.ShapeDtypeStruct((2, 4, 4, 4, shard, width), BF16),
            jax.ShapeDtypeStruct((2, 4, 4, 4, shard, rank), BF16),
            jax.ShapeDtypeStruct((1, total), F32),
        ),
        in_specs=[anywhere, anywhere, vmem],
        out_specs=(anywhere, vmem, anywhere, anywhere, anywhere),
        scratch_shapes=[
            pltpu.VMEM((2, 4, 4, 4, shard, width), BF16),
            pltpu.VMEM((2, 4, 4, 4, shard, rank), BF16),
            pltpu.VMEM((1, total), F32),
            pltpu.VMEM((2, 256, total), BF16),
            pltpu.VMEM((256, 128), F32),
            dma((2,)), dma((48,)), dma((48,)), dma((40,)), dma((40,)), dma((3,)), dma((2,)),
        ],
        compiler_params=pltpu.CompilerParams(
            collective_id=0, has_side_effects=True, vmem_limit_bytes=VMEM_LIMIT
        ),
    )(landmarks, initial_basis, points)

    own, spectral = pl.pallas_call(
        functools.partial(main_kernel, scale),
        name="eigenbasis",
        out_shape=(
            jax.ShapeDtypeStruct((shard, rank), F32),
            jax.ShapeDtypeStruct((total, rank), BF16),
        ),
        in_specs=[anywhere, anywhere, vmem],
        out_specs=(vmem, anywhere),
        scratch_shapes=[
            pltpu.VMEM((half, total), F32),
            pltpu.VMEM((2, total, rank), BF16),
            pltpu.VMEM((2, 8, total), F32),
            pltpu.VMEM((2, 2, rank, rank), F32),
            pltpu.VMEM((rank, 2 * rank), F32),
            pltpu.VMEM((rank, rank), F32),
            pltpu.VMEM((rank, rank), F32),
            pltpu.VMEM((half, 1), F32),
            pltpu.VMEM((1, total), F32),
            pltpu.VMEM((256, 512), F32),
            pltpu.VMEM((half, rank), BF16),
            dma((2,)), dma((2, 1)), dma((2, 2)), dma((2, 2)), dma((2, 1)), dma,
        ],
        compiler_params=pltpu.CompilerParams(
            collective_id=1, has_side_effects=True, vmem_limit_bytes=VMEM_LIMIT
        ),
    )(land.reshape(total, width), basis.reshape(total, rank), sq)

    coords = pl.pallas_call(
        coords_kernel,
        name="coords",
        grid=(count // 256,),
        out_shape=jax.ShapeDtypeStruct((count, rank), F32),
        in_specs=[
            pl.BlockSpec((256, total), lambda i: (i, 0)),
            pl.BlockSpec((total, rank), lambda i: (0, 0)),
            pl.BlockSpec((256, 1), lambda i: (i, 0)),
        ],
        out_specs=pl.BlockSpec((256, rank), lambda i: (i, 0)),
    )(weights, spectral, factor)
    return own, coords


def solution(mesh):
    in_specs = (P(("grp", "row"), None), P(("grp", "row"), None), P(("grp", "row"), None))
    out_specs = (P(("grp", "row"), None), P(("grp", "row"), None))
    return jax.shard_map(body, mesh=mesh, in_specs=in_specs, out_specs=out_specs, check_vma=False)
```

time: 815 us -> 164 us (0.20)
  waiting for transfers between devices: 517 us -> 0 us
  Pallas kernels: 0 us -> 163 us
  other arithmetic: 122 us -> 0 us
  blocking collectives: 59.6 us -> 0 us
  starting transfers between devices: 43.6 us -> 0 us
  matrix products: 29.3 us -> 0 us
  local copies, waits for them, and re-layouts: 19.8 us -> 0.62 us
  between operations: 18.6 us -> 0.66 us
    psum x2 -> x0, waiting for transfers between devices: 324 us -> none  [body(): lax.psum(jnp.dot(image.T, image, precision=lax.Precision.HIGHEST), ('grp'...]
    pallas_call x0 -> x3, Pallas kernels: none -> 163 us  [the longest x1 86.8 us: body(): pl.pallas_call(functools.partial(main_kernel, scale), name='eigenbasis',...]
    all_gather x2 -> x0, waiting for transfers between devices: 123 us -> none  [the longest x1 123 us: body(): group_rows = lax.all_gather(landmarks, 'row', axis=0, tiled=True)]
    another operation x18 -> x0, other arithmetic: 108 us -> none  [the longest x13 68.6 us: body(): lower = jnp.linalg.cholesky(gram)]
    all_to_all x4 -> x0, blocking collectives: 59.6 us -> none  [the longest x2 38.7 us: sum_at_owner(): blocks = lax.all_to_all(in_blocks(x, dim, devices), axis, 0, 0, tiled=True)]
    reduce_scatter x1 -> x0, waiting for transfers between devices: 52.7 us -> none  [side_by_side(): lax.psum_scatter(both, axis, scatter_dimension=dim, tiled=True)]
    all_to_all x4 -> x0, starting transfers between devices: 43.2 us -> none  [copy_for_each(): lax.all_to_all(jnp.broadcast_to(x[None], (devices, *x.shape)), axis, 0, 0...]
    dot_general x7 -> x0, matrix products: 27.3 us -> none  [the longest x1 13.9 us: point_terms(): lax.dot_general(anchors, members, (((1,), (1,)), ((), ())), preferred_ele...]
  transfers between devices with their start and end apart: 9 -> 0, of which waited for: 7 -> 0; matrix products, arithmetic and copies ran while one was open for 11% -> 0% of each run, Pallas kernels for 0% -> 0%
where the time goes in v1:
time: 164 us
  Pallas kernels  163 us (99%)
    pallas_call x1, Pallas kernels, body(): pl.pallas_call(functools.partial(main_kernel, scale), name='eigenbasis',...  86.8 us
    pallas_call x1, Pallas kernels, body(): pl.pallas_call(functools.partial(gather_kernel, scale), name='gather', ou...  68.2 us
    pallas_call x1, Pallas kernels, body(): pl.pallas_call(coords_kernel, name='coords', grid=(count // 256,), out_sh...  7.68 us

profile of v1, /device:TPU:1, one launch (start us, length us, event | category | flops | bytes accessed | tf_op | source)
XLA Modules:
  0.0 163.9 jit_solution(11866633101822045431)
XLA Ops:
  0.6 68.2 %gather.1 = (bf16[1024,4096]{1,0:T(8,128)(2,1)}, f32[1024,1]{1,0:T(8,128)}, bf16[2,4,4,4,32,1024]{5,4,3,2,1,0:T(8,128)(2,1)}, bf16[2,4,4,4,32,256]{5,4,3,2,1,0:T(8,128)(2,1)}, f32[1,4096]{1,0:T(1,128)}) custom-call(bf16[32,1024]{1,0:T(8,128)(2,1)} %land_in.1, bf16[32,256]{1,0:T(8,128)(2,1)} %basis_in.1, bf16[1024,1024]{1,0:T(8,128)(2,1)} %points_ref.1), custom_call_target="tpu_custom_call" | custom-call | tf_op jit(solution)/shard_map/gather/pallas_call | solution.py:384
  68.8 86.8 %eigenbasis.1 = (f32[32,256]{1,0:T(8,128)}, bf16[4096,256]{1,0:T(8,128)(2,1)}) custom-call(bf16[4096,1024]{1,0:T(8,128)(2,1)} %bitcast.2, bf16[4096,256]{1,0:T(8,128)(2,1)} %bitcast.3, f32[1,4096]{1,0:T(1,128)} %get-tuple-element.11.sq_ref), custom_call_target="tpu_custom_call" | custom-call | tf_op jit(solution)/shard_map/eigenbasis/pallas_call | solution.py:409
  155.6 0.0 copy-start
  155.6 7.7 %coords.1 = f32[1024,256]{1,0:T(8,128)} custom-call(bf16[1024,4096]{1,0:T(8,128)(2,1)} %get-tuple-element.13.weights_ref, bf16[4096,256]{1,0:T(8,128)(2,1)} %get-tuple-element.14.spectral_ref, f32[1024,1]{1,0:T(8,128)} %get-tuple-element.15.factor_ref), custom_call_target="tpu_custom_call" | custom-call | tf_op jit(solution)/shard_map/coords/pallas_call | solution.py:437
  163.3 0.0 copy-done
  163.3 0.6 copy.6
Async XLA Ops:
  155.6 7.7 %copy-start = (f32[32,256]{1,0:T(8,128)S(1)}, f32[32,256]{1,0:T(8,128)}, u32[]{:S(2)}) copy-start(f32[32,256]{1,0:T(8,128)} %get-tuple-element.18) | copy-start | bytes 98308

commit v2 on v0

v2 whole, which is shorter than its diff:
```python
import functools
import math

import jax
import jax.numpy as jnp
from jax import lax
from jax.experimental import pallas as pl
from jax.experimental.pallas import tpu as pltpu
from jax.sharding import PartitionSpec as P

ITERS = 2
SPREAD = 0.25
LOG2E = 1.4426950408889634
MESH = pl.DeviceIdType.MESH
F32 = jnp.float32
BF16 = jnp.bfloat16
VMEM_LIMIT = 67_043_328


def place():
    grp, row = lax.axis_index("grp"), lax.axis_index("row")
    core, y_hi = lax.rem(grp, 2), grp // 2
    y_lo, z, x = row // 16, lax.rem(row // 4, 4), lax.rem(row, 4)
    return core, {"z": z, "y": y_hi * 2 + y_lo, "x": x}


def device(core, at):
    return ((at["y"] // 2) * 2 + core, lax.rem(at["y"], 2) * 16 + at["z"] * 4 + at["x"])


def neighbour(core, at, axis, by):
    return device(core, {**at, axis: lax.rem(at[axis] + by + 4, 4)})


def dot_nt(a, b):
    return lax.dot_general(a, b, (((1,), (1,)), ((), ())), preferred_element_type=F32)


def dot_tn(a, b):
    return lax.dot_general(a, b, (((0,), (0,)), ((), ())), preferred_element_type=F32)


ORDERS = (("x", "y", "z"), ("y", "z", "x"), ("z", "x", "y"))


def nystrom_kernel(
    scale, land_in, basis_in, points_in,
    own_out, coords_out, weights_out,
    land, xs, norms, kern, upper, image, sq, csum, grams, aug, lower_t, inverse,
    col_scale, row_scale, factor,
    own_sem, send_sem, recv_sem, fsend, frecv, w_sem, c_sem, g_sem, x_sem, s_sem, o_sem,
):
    core, at = place()
    partner = device(1 - core, at)
    own = (core, at["z"], at["y"], at["x"])
    half = kern.shape[0]
    count = points_in.shape[0]

    first = [
        pltpu.make_async_copy(land_in, land.at[own], own_sem.at[0]),
        pltpu.make_async_copy(basis_in, xs.at[(0, *own)], own_sem.at[1]),
    ]
    for c in first:
        c.start()
    points = upper.at[:, pl.ds(0, 1024)]
    points_copy = pltpu.make_async_copy(points_in, points, own_sem.at[2])
    points_copy.start()
    barrier = pltpu.get_barrier_semaphore()
    peers = [neighbour(core, at, a, by) for a in "xyz" for by in (1, -1)] + [partner]
    for peer in peers:
        pl.semaphore_signal(barrier, inc=1, device_id=peer, device_id_type=MESH)
    for c in first:
        c.wait()
    mine = land[own].astype(F32)
    own_sq = jnp.sum(mine * mine, axis=1, keepdims=True) * scale
    lane = lax.broadcasted_iota(jnp.int32, (32, 128), 1)
    row = lax.broadcasted_iota(jnp.int32, (32, 128), 0)
    norms[own] = jnp.sum(jnp.where(lane == row + at["x"] * 32, own_sq, 0.0), axis=0, keepdims=True)
    pl.semaphore_wait(barrier, len(peers))

    everything = slice(None)
    stages = []
    for s in range(2):
        rows = pl.ds(16 * s, 16)
        stages.append([
            (land, (), rows, pl.ds(0, 384), ORDERS[0]),
            (land, (), rows, pl.ds(384, 384), ORDERS[1]),
            (land, (), rows, pl.ds(768, 256), ORDERS[2]),
            (xs, (0,), rows, pl.ds(0, 128), ORDERS[2]),
            (xs, (0,), rows, pl.ds(128, 128), ORDERS[s]),
        ])
    stages[1].append((norms, (), everything, everything, ORDERS[2]))

    def block(part, phase, shift):
        buf, lead, rows, cols, order = part
        index = [*lead, core]
        for a in "zyx":
            if a == order[phase]:
                index.append(lax.rem(at[a] + shift + 4, 4))
            elif a in order[:phase]:
                index.append(everything)
            else:
                index.append(at[a])
        return buf.at[tuple(index + [rows, cols])]

    sent, forwarded = [], []

    def send(ref, dev):
        k = len(sent)
        c = pltpu.make_async_remote_copy(
            src_ref=ref, dst_ref=ref, send_sem=send_sem.at[k], recv_sem=recv_sem.at[k],
            device_id=dev, device_id_type=MESH,
        )
        c.start()
        sent.append(c)
        return c

    def forward(ref):
        k = len(forwarded)
        c = pltpu.make_async_remote_copy(
            src_ref=ref, dst_ref=ref, send_sem=fsend.at[k], recv_sem=frecv.at[k],
            device_id=partner, device_id_type=MESH,
        )
        c.start()
        forwarded.append(c)

    def near(part, phase):
        a = part[4][phase]
        ref = block(part, phase, 0)
        return send(ref, neighbour(core, at, a, 1)), send(ref, neighbour(core, at, a, -1))

    def far(s, part, phase, arrivals):
        a = part[4][phase]
        below, above = arrivals
        if s == 0:
            below.wait_recv()
            c = send(block(part, phase, -1), neighbour(core, at, a, 1))
            above.wait_recv()
        else:
            above.wait_recv()
            c = send(block(part, phase, 1), neighbour(core, at, a, -1))
            below.wait_recv()
        forward(block(part, phase, -1))
        forward(block(part, phase, 1))
        return c

    def finish(part, phase, c):
        c.wait_recv()
        forward(block(part, phase, 2))

    far_sent = [None, None]
    for phase in range(3):
        near_sent = [None, None]
        for s, parts in enumerate(stages):
            if phase:
                for part, c in zip(parts, far_sent[s]):
                    finish(part, phase - 1, c)
            near_sent[s] = [near(part, phase) for part in parts]
            if not phase:
                for part in parts:
                    forward(block(part, 0, 0))
        for s, parts in enumerate(stages):
            far_sent[s] = [far(s, part, phase, n) for part, n in zip(parts, near_sent[s])]
    for s, parts in enumerate(stages):
        for part, c in zip(parts, far_sent[s]):
            finish(part, 2, c)
    for c in forwarded:
        c.wait_recv()

    for b in range(32):
        c, z, y = b // 16, b // 4 % 4, b % 4
        lines = norms[c, z, y]
        sq[:, b * 128 : (b + 1) * 128] = lines[0] + lines[1] + lines[2] + lines[3]

    points_copy.wait()
    wide = points[...].astype(F32)
    factor[...] = jnp.sum(wide * wide, axis=1, keepdims=True) * scale
    image[:count, 128:] = jnp.zeros((count, 128), F32)

    def weights_copy(j, slot):
        return pltpu.make_async_copy(
            upper.at[:, pl.ds(pl.multiple_of(1024 + slot * 512, 512), 512)],
            weights_out.at[:, pl.ds(pl.multiple_of(j * 512, 512), 512)],
            w_sem.at[slot],
        )

    def point_chunk(j, _):
        slot = lax.rem(j, 2)

        @pl.when(j >= 2)
        def _():
            weights_copy(j - 2, slot).wait()

        rows = land[j // 4, lax.rem(j, 4)].reshape(512, 1024)
        cols = pl.ds(pl.multiple_of(j * 512, 512), 512)
        close = jnp.exp2(dot_nt(points[...], rows) * (2.0 * scale) - (factor[...] + sq[:, cols]))
        upper[:, pl.ds(pl.multiple_of(1024 + slot * 512, 512), 512)] = close.astype(BF16)
        image[:count, 128:] += close[:, :128] + close[:, 128:256] + close[:, 256:384] + close[:, 384:]
        weights_copy(j, slot).start()
        return 0

    lax.fori_loop(0, 8, point_chunk, 0)
    factor[...] = 64.0 / jnp.sqrt(jnp.sum(image[:count, 128:], axis=1, keepdims=True))

    csum[0] = jnp.zeros(csum.shape[1:], F32)
    image[:, :128] = jnp.zeros((half, 128), F32)
    for z in range(4):
        wide = land[core, z].reshape(512, 1024).astype(F32)
        col_scale[z * 512 : (z + 1) * 512, :] = jnp.sum(wide * wide, axis=1, keepdims=True) * scale

    def land_chunk(j, _):
        rows = land[j // 8, lax.rem(j // 2, 4), pl.ds(lax.rem(j, 2) * 2, 2)].reshape(256, 1024)
        cols = pl.ds(pl.multiple_of(j * 256, 256), 256)
        inner = dot_nt(land[core].reshape(half, 1024), rows)
        close = jnp.exp2(inner * (2.0 * scale) - (col_scale[...] + sq[:, cols]))
        kern[:, cols] = close
        image[:, :128] += close[:, :128] + close[:, 128:]
        csum[0, :, cols] += jnp.sum(close.reshape(half // 8, 8, 256), axis=0)
        return 0

    lax.fori_loop(0, 16, land_chunk, 0)

    def swap(src, dst, sems, index):
        c = pltpu.make_async_remote_copy(
            src_ref=src, dst_ref=dst, send_sem=sems.at[0, index], recv_sem=sems.at[1, index],
            device_id=partner, device_id_type=MESH,
        )
        c.start()
        return c

    give = swap(csum.at[0], csum.at[1], c_sem, 0)
    col_scale[...] = 1.0 / jnp.sqrt(jnp.sum(image[:, :128], axis=1, keepdims=True))
    give.wait_recv()
    row_scale[...] = 1.0 / jnp.sqrt(jnp.sum(csum[0] + csum[1], axis=0, keepdims=True))
    weights_copy(6, 0).wait()
    weights_copy(7, 1).wait()
    for c in sent:
        c.wait_send()
    for c in forwarded:
        c.wait_send()
    give.wait_send()

    eye = lax.broadcasted_iota(jnp.int32, (256, 256), 0) == lax.broadcasted_iota(jnp.int32, (256, 256), 1)
    pending = []
    for step in range(ITERS):
        last = step == ITERS - 1

        def lower_tile(t, _):
            r = pl.ds(pl.multiple_of(t * 512, 512), 512)
            pieces = []
            for c in range(4):
                place_at = (c // 2, c % 2 * 2 + t)
                if step == 0:
                    cols = pl.ds(c * 1024, 1024)
                    piece = (kern[r, cols] * col_scale[r, :] * row_scale[:, cols]).astype(BF16)
                    land[place_at] = piece.reshape(4, 4, 32, 1024)
                pieces.append(land[place_at].reshape(512, 1024))
            rows = jnp.concatenate(pieces, axis=1)
            image[r, :] = jnp.dot(rows, xs[step].reshape(2 * half, 256), preferred_element_type=F32)
            return 0

        def upper_tile(t, _):
            r = pl.ds(pl.multiple_of(1024 + t * 512, 512), 512)
            u = pl.ds(pl.multiple_of(t * 512, 512), 512)
            if step == 0:
                for c in range(4):
                    cols = pl.ds(c * 1024, 1024)
                    upper[u, cols] = (kern[r, cols] * col_scale[r, :] * row_scale[:, cols]).astype(BF16)
            image[r, :] = jnp.dot(upper[u, :], xs[step].reshape(2 * half, 256), preferred_element_type=F32)
            return 0

        lax.fori_loop(0, 2, upper_tile, 0)
        if last:
            weights_in = pltpu.make_async_copy(weights_out, upper, w_sem.at[0])
            weights_in.start()
        lax.fori_loop(0, 2, lower_tile, 0)
        hi, lo = split(image[...])
        gram = dot_tn(hi, jnp.concatenate([hi, lo], axis=1))
        cross = gram[:, 256:]
        grams[step, 0] = gram[:, :256] + cross + cross.T
        give = swap(grams.at[step, 0], grams.at[step, 1], g_sem, step)
        aug[:, 256:] = jnp.where(eye, 1.0, 0.0)
        give.wait_recv()
        aug[:, :256] = grams[step, 0] + grams[step, 1]
        pending.append(give)
        cholesky_inverse(aug, lower_t, inverse)
        ihi, ilo = split(inverse[...])
        stacked = jnp.concatenate([ihi, ilo, ihi], axis=1)
        if last:
            inverse_lam = 1.0 / jnp.sum(jnp.where(eye, lower_t[...], 0.0), axis=0, keepdims=True)
        gives = []
        target = 0 if last else step + 1
        for t in range(2):
            r = pl.ds(t * 1024, 1024)
            hi, lo = split(image[r, :])
            ortho = dot_nt(jnp.concatenate([hi, hi, lo], axis=1), stacked)
            if last:
                image[r, :] = ortho
                ortho = ortho * col_scale[r, :] * inverse_lam
            xs[target, core, 2 * t : 2 * t + 2] = ortho.astype(BF16).reshape(2, 4, 4, 32, 256)
            part = xs.at[target, core, pl.ds(2 * t, 2)]
            gives.append(swap(part, part, s_sem if last else x_sem, t))
        if last:
            index = at["z"] * 16 + at["y"] * 4 + at["x"]
            own_out[...] = image[pl.ds(pl.multiple_of(index * 32, 32), 32), :]
            weights_in.wait()
        for c in gives:
            c.wait_recv()
        pending += gives

    copies = []
    for t in range(2):
        r = pl.ds(t * 512, 512)
        numer = jnp.dot(upper[r, :], xs[0].reshape(2 * half, 256), preferred_element_type=F32)
        image[r, :] = numer * factor[r, :]
        copies.append(pltpu.make_async_copy(image.at[r, :], coords_out.at[r, :], o_sem.at[t]))
        copies[-1].start()
    for c in pending:
        c.wait_send()
    for c in copies:
        c.wait()


def split(x):
    hi = x.astype(BF16)
    return hi, (x - hi.astype(F32)).astype(BF16)


def cholesky_inverse(aug, lower_t, inverse):
    lane = 128
    row_id = lax.broadcasted_iota(jnp.int32, (16, lane), 0)
    for b in range(16):
        r0 = b * 16
        diag = aug[pl.ds(r0, 16), :256]
        reps = [jnp.broadcast_to(diag[:, r0 + j : r0 + j + 1], (16, lane)) for j in range(16)]
        panel = [aug[pl.ds(r0, 16), pl.ds(k * lane, lane)] for k in range(4)]
        for j in range(16):
            root = lax.rsqrt(reps[j][j : j + 1, :])
            column = reps[j] * root
            for i in range(j + 1, 16):
                reps[i] = reps[i] - column * column[i : i + 1, :]
            below = jnp.where(row_id > j, column, 0.0)
            for k in range(4):
                line = panel[k][j : j + 1, :] * root
                panel[k] = jnp.where(row_id == j, line, panel[k] - below * line)
        for k in range(2):
            lower_t[pl.ds(r0, 16), pl.ds(k * lane, lane)] = panel[k]
            inverse[pl.ds(r0, 16), pl.ds(k * lane, lane)] = panel[2 + k]
        if b < 15:
            rows = jnp.concatenate(panel, axis=1)
            hi = rows.astype(BF16)
            rest = rows - hi.astype(F32)
            mid = rest.astype(BF16)
            low = (rest - mid.astype(F32)).astype(BF16)
            left = jnp.concatenate([hi, hi, mid, mid, hi, low], axis=0)[:, :256]
            right = jnp.concatenate([hi, mid, hi, mid, low, hi], axis=0)
            start = (r0 + 16) // 128 * 128
            aug[start:, :] = aug[start:, :] - dot_tn(left[:, start:], right)


def body(landmarks, initial_basis, points):
    shard, width = landmarks.shape
    rank = initial_basis.shape[1]
    total = shard * 128
    half = total // 2
    count = points.shape[0]
    scale = LOG2E / (SPREAD * width)
    anywhere = pl.BlockSpec(memory_space=pl.ANY)
    vmem = pl.BlockSpec(memory_space=pltpu.VMEM)
    dma = pltpu.SemaphoreType.DMA

    own, coords, _ = pl.pallas_call(
        functools.partial(nystrom_kernel, scale),
        name="nystrom",
        out_shape=(
            jax.ShapeDtypeStruct((shard, rank), F32),
            jax.ShapeDtypeStruct((count, rank), F32),
            jax.ShapeDtypeStruct((count, total), BF16),
        ),
        in_specs=[anywhere, anywhere, anywhere],
        out_specs=(vmem, anywhere, anywhere),
        scratch_shapes=[
            pltpu.VMEM((2, 4, 4, 4, shard, width), BF16),
            pltpu.VMEM((2, 2, 4, 4, 4, shard, rank), BF16),
            pltpu.VMEM((2, 4, 4, 4, 1, 128), F32),
            pltpu.VMEM((half, total), F32),
            pltpu.VMEM((count, total), BF16),
            pltpu.VMEM((half, rank), F32),
            pltpu.VMEM((1, total), F32),
            pltpu.VMEM((2, 8, total), F32),
            pltpu.VMEM((2, 2, rank, rank), F32),
            pltpu.VMEM((rank, 2 * rank), F32),
            pltpu.VMEM((rank, rank), F32),
            pltpu.VMEM((rank, rank), F32),
            pltpu.VMEM((half, 1), F32),
            pltpu.VMEM((1, total), F32),
            pltpu.VMEM((count, 1), F32),
            dma((3,)), dma((99,)), dma((99,)), dma((110,)), dma((110,)), dma((2,)),
            dma((2, 1)), dma((2, 2)), dma((2, 2)), dma((2, 2)), dma((2,)),
        ],
        compiler_params=pltpu.CompilerParams(
            collective_id=0, has_side_effects=True, vmem_limit_bytes=VMEM_LIMIT
        ),
    )(landmarks, initial_basis, points)
    return own, coords


def solution(mesh):
    in_specs = (P(("grp", "row"), None), P(("grp", "row"), None), P(("grp", "row"), None))
    out_specs = (P(("grp", "row"), None), P(("grp", "row"), None))
    return jax.shard_map(body, mesh=mesh, in_specs=in_specs, out_specs=out_specs, check_vma=False)
```

time: 815 us -> 127 us (0.16)
  waiting for transfers between devices: 517 us -> 0 us
  Pallas kernels: 0 us -> 122 us
  other arithmetic: 122 us -> 0 us
  blocking collectives: 59.6 us -> 0 us
  starting transfers between devices: 43.6 us -> 0 us
  matrix products: 29.3 us -> 0 us
  between operations: 18.6 us -> 0.64 us
  local copies, waits for them, and re-layouts: 19.8 us -> 3.64 us
    psum x2 -> x0, waiting for transfers between devices: 324 us -> none  [body(): lax.psum(jnp.dot(image.T, image, precision=lax.Precision.HIGHEST), ('grp'...]
    all_gather x2 -> x0, waiting for transfers between devices: 123 us -> none  [the longest x1 123 us: body(): group_rows = lax.all_gather(landmarks, 'row', axis=0, tiled=True)]
    pallas_call x0 -> x1, Pallas kernels: none -> 122 us  [body(): pl.pallas_call(functools.partial(nystrom_kernel, scale), name='nystrom',...]
    another operation x18 -> x0, other arithmetic: 108 us -> none  [the longest x13 68.6 us: body(): lower = jnp.linalg.cholesky(gram)]
    all_to_all x4 -> x0, blocking collectives: 59.6 us -> none  [the longest x2 38.7 us: sum_at_owner(): blocks = lax.all_to_all(in_blocks(x, dim, devices), axis, 0, 0, tiled=True)]
    reduce_scatter x1 -> x0, waiting for transfers between devices: 52.7 us -> none  [side_by_side(): lax.psum_scatter(both, axis, scatter_dimension=dim, tiled=True)]
    all_to_all x4 -> x0, starting transfers between devices: 43.2 us -> none  [copy_for_each(): lax.all_to_all(jnp.broadcast_to(x[None], (devices, *x.shape)), axis, 0, 0...]
    dot_general x7 -> x0, matrix products: 27.3 us -> none  [the longest x1 13.9 us: point_terms(): lax.dot_general(anchors, members, (((1,), (1,)), ((), ())), preferred_ele...]
  transfers between devices with their start and end apart: 9 -> 0, of which waited for: 7 -> 0; matrix products, arithmetic and copies ran while one was open for 11% -> 0% of each run, Pallas kernels for 0% -> 0%
where the time goes in v2:
time: 127 us
  Pallas kernels  122 us (96%)
  local copies, waits for them, and re-layouts  3.64 us (3%)
    pallas_call x1, Pallas kernels, body(): pl.pallas_call(functools.partial(nystrom_kernel, scale), name='nystrom',...  122 us
    unnamed x2, local copies, waits for them, and re-layouts  3.64 us

profile of v2, /device:TPU:1, one launch (start us, length us, event | category | flops | bytes accessed | tf_op | source)
XLA Modules:
  0.0 126.7 jit_solution(12664957287692914714)
XLA Ops:
  0.6 122.4 %nystrom.1 = (f32[32,256]{1,0:T(8,128)}, f32[1024,256]{1,0:T(8,128)}, bf16[1024,4096]{1,0:T(8,128)(2,1)}) custom-call(bf16[32,1024]{1,0:T(8,128)(2,1)} %land_in.1, bf16[32,256]{1,0:T(8,128)(2,1)} %basis_in.1, bf16[1024,1024]{1,0:T(8,128)(2,1)} %points_in.1), custom_call_target="tpu_custom_call" | custom-call | tf_op jit(solution)/shard_map/nystrom/pallas_call | solution.py:372
  123.1 1.4 %copy.7 = f32[32,256]{1,0:T(8,128)} copy(f32[32,256]{1,0:T(8,128)} %get-tuple-element.8) | data formatting | bytes 65536
  124.4 2.3 %copy.8 = f32[1024,256]{1,0:T(8,128)} copy(f32[1024,256]{1,0:T(8,128)} %get-tuple-element.9) | data formatting | bytes 2097152

commit v3 on v2

v3 whole, which is shorter than its diff:
```python
import functools
import math

import jax
import jax.numpy as jnp
from jax import lax
from jax.experimental import pallas as pl
from jax.experimental.pallas import tpu as pltpu
from jax.sharding import PartitionSpec as P

ITERS = 2
SPREAD = 0.25
LOG2E = 1.4426950408889634
MESH = pl.DeviceIdType.MESH
F32 = jnp.float32
BF16 = jnp.bfloat16
VMEM_LIMIT = 67_043_328


def place():
    grp, row = lax.axis_index("grp"), lax.axis_index("row")
    core, y_hi = lax.rem(grp, 2), grp // 2
    y_lo, z, x = row // 16, lax.rem(row // 4, 4), lax.rem(row, 4)
    return core, {"z": z, "y": y_hi * 2 + y_lo, "x": x}


def device(core, at):
    return ((at["y"] // 2) * 2 + core, lax.rem(at["y"], 2) * 16 + at["z"] * 4 + at["x"])


def neighbour(core, at, axis, by):
    return device(core, {**at, axis: lax.rem(at[axis] + by + 4, 4)})


def dot_nt(a, b):
    return lax.dot_general(a, b, (((1,), (1,)), ((), ())), preferred_element_type=F32)


def dot_tn(a, b):
    return lax.dot_general(a, b, (((0,), (0,)), ((), ())), preferred_element_type=F32)


ORDERS = (("x", "y", "z"), ("y", "z", "x"), ("z", "x", "y"))
EVERY = slice(None)


def split(x):
    hi = x.astype(BF16)
    return hi, (x - hi.astype(F32)).astype(BF16)


def in_three(x):
    hi = x.astype(BF16)
    rest = x - hi.astype(F32)
    mid = rest.astype(BF16)
    return hi, mid, (rest - mid.astype(F32)).astype(BF16)


def cholesky_inverse(aug, lower_t, inverse):
    lane, size = 128, 32
    row_id = lax.broadcasted_iota(jnp.int32, (size, lane), 0)
    for r0 in range(0, 256, size):
        end = r0 + size
        diag = aug[pl.ds(r0, size), :256]
        reps = [jnp.broadcast_to(diag[:, r0 + j : r0 + j + 1], (size, lane)) for j in range(size)]
        panel = [aug[pl.ds(r0, size), pl.ds(k * lane, lane)] for k in range(4)]
        live = [k for k in range(4) if (k < 2 and (k + 1) * lane > r0) or (k >= 2 and (k - 2) * lane < end)]
        for j in range(size):
            root = lax.rsqrt(reps[j][j : j + 1, :])
            column = reps[j] * root
            for i in range(j + 1, size):
                reps[i] = reps[i] - column * column[i : i + 1, :]
            below = jnp.where(row_id > j, column, 0.0)
            for k in live:
                line = panel[k][j : j + 1, :] * root
                panel[k] = jnp.where(row_id == j, line, panel[k] - below * line)
        for k in range(2):
            lower_t[pl.ds(r0, size), pl.ds(k * lane, lane)] = panel[k]
            inverse[pl.ds(r0, size), pl.ds(k * lane, lane)] = panel[2 + k]
        if end < 256:
            start = end // lane * lane
            after = [k for k in range(4) if (k < 2 and k * lane >= start) or (k >= 2 and (k - 2) * lane < end)]
            terms = [in_three(panel[k]) for k in range(4)]

            def stack(columns, order):
                return jnp.concatenate(
                    [jnp.concatenate([terms[k][o] for o in order], axis=0) for k in columns], axis=1
                )

            left = stack(range(start // lane, 2), (0, 0, 1, 1, 0, 2))
            change = dot_tn(left, stack(after, (0, 1, 0, 1, 2, 0)))
            for n, k in enumerate(after):
                cols = pl.ds(k * lane, lane)
                aug[start:, cols] = aug[start:, cols] - change[:, n * lane : (n + 1) * lane]


def nystrom_kernel(
    scale, land_in, basis_in, points_in,
    own_out, coords_out, weights_out,
    land, xs, norms, kern, upper, image, sq, csum, grams, aug, lower_t, inverse,
    col_scale, row_scale, factor,
    own_sem, send_sem, recv_sem, fsend, frecv, w_sem, c_sem, g_sem, x_sem, s_sem, o_sem,
):
    core, at = place()
    partner = device(1 - core, at)
    own = (core, at["z"], at["y"], at["x"])
    half = kern.shape[0]
    count = points_in.shape[0]

    first = []
    for s in range(2):
        rows = pl.ds(16 * s, 16)
        first.append(pltpu.make_async_copy(land_in.at[rows, :], land.at[(s, *own)], own_sem.at[s]))
        first.append(pltpu.make_async_copy(basis_in.at[rows, :], xs.at[(0, s, *own)], own_sem.at[2 + s]))
    for c in first:
        c.start()
    points = upper.at[:, pl.ds(0, 1024)]
    points_copy = pltpu.make_async_copy(points_in, points, own_sem.at[4])
    points_copy.start()
    barrier = pltpu.get_barrier_semaphore()
    peers = [neighbour(core, at, a, by) for a in "xyz" for by in (1, -1, 2)] + [partner]
    for peer in peers:
        pl.semaphore_signal(barrier, inc=1, device_id=peer, device_id_type=MESH)
    for c in first:
        c.wait()
    offset = lax.rem(at["y"], 2) * 64 + at["x"] * 16
    spot = lax.broadcasted_iota(jnp.int32, (16, 128), 1) == lax.broadcasted_iota(jnp.int32, (16, 128), 0) + offset
    lines = []
    for s in range(2):
        mine = land[(s, *own)].astype(F32)
        own_sq = jnp.sum(mine * mine, axis=1, keepdims=True) * scale
        lines.append(jnp.sum(jnp.where(spot, own_sq, 0.0), axis=0, keepdims=True))
    norms[own] = jnp.concatenate(lines, axis=0)
    pl.semaphore_wait(barrier, len(peers))

    stages = []
    for s in range(2):
        stages.append([
            (land, (s,), pl.ds(0, 384), ORDERS[0]),
            (land, (s,), pl.ds(384, 384), ORDERS[1]),
            (land, (s,), pl.ds(768, 256), ORDERS[2]),
        ])
    stages[0].append((norms, (), EVERY, ORDERS[2]))
    late = [(xs, (0, 0), EVERY, ORDERS[0]), (xs, (0, 1), EVERY, ORDERS[1])]

    def block(part, phase, shift):
        buf, lead, cols, order = part
        index = [*lead, core]
        for a in "zyx":
            if a == order[phase]:
                index.append(lax.rem(at[a] + shift + 4, 4))
            elif a in order[:phase]:
                index.append(EVERY)
            else:
                index.append(at[a])
        return buf.at[tuple(index + [EVERY, cols])]

    sent, forwarded = [], []

    def send(part, phase, shift, by):
        k = len(sent)
        ref = block(part, phase, shift)
        c = pltpu.make_async_remote_copy(
            src_ref=ref, dst_ref=ref, send_sem=send_sem.at[k], recv_sem=recv_sem.at[k],
            device_id=neighbour(core, at, part[3][phase], by), device_id_type=MESH,
        )
        c.start()
        sent.append(c)
        return c

    def forward(part, phase, shift):
        k = len(forwarded)
        ref = block(part, phase, shift)
        c = pltpu.make_async_remote_copy(
            src_ref=ref, dst_ref=ref, send_sem=fsend.at[k], recv_sem=frecv.at[k],
            device_id=partner, device_id_type=MESH,
        )
        c.start()
        forwarded.append(c)
        return c

    def around(parts, phase):
        return [send(part, phase, 0, by) for by in (2, 1, -1) for part in parts]

    def receive(copies):
        for c in copies:
            c.wait_recv()

    ring = [around(parts, 0) for parts in stages]
    points_copy.wait()
    wide = points[...].astype(F32)
    factor[...] = jnp.sum(wide * wide, axis=1, keepdims=True) * scale
    image[...] = jnp.zeros_like(image)
    csum[0] = jnp.zeros(csum.shape[1:], F32)
    for s, parts in enumerate(stages):
        receive(ring[s])
        ring[s] = around(parts, 1)
    here, there = stages
    handed = [[], []]
    receive(ring[0])
    here_up = [send(part, 2, 0, 1) for part in here]
    here_down = [send(part, 2, 0, -1) for part in here]
    handed[0] += [forward(part, 2, 0) for part in here]
    receive(ring[1])
    there_down = [send(part, 2, 0, -1) for part in there]
    handed[1] += [forward(part, 2, 0) for part in there]
    here_far = []
    for part, c in zip(here, here_up):
        c.wait_recv()
        here_far.append(send(part, 2, -1, 1))
    there_up = [send(part, 2, 0, 1) for part in there]
    handed[0] += [forward(part, 2, -1) for part in here]
    receive(here_down)
    handed[0] += [forward(part, 2, 1) for part in here]
    there_far = []
    for part, c in zip(there, there_down):
        c.wait_recv()
        there_far.append(send(part, 2, 1, -1))
    handed[1] += [forward(part, 2, 1) for part in there]
    for part, c in zip(here, here_far):
        c.wait_recv()
        handed[0].append(forward(part, 2, 2))
    late_ring = around(late, 0)

    def own_norms(s):
        wide = land[s, core].reshape(half // 2, 1024).astype(F32)
        rows = pl.ds(s * (half // 2), half // 2)
        col_scale[rows, :] = jnp.sum(wide * wide, axis=1, keepdims=True) * scale

    own_norms(0)
    receive(handed[0])
    for c in range(2):
        for z in range(4):
            for pair in range(2):
                lines = norms[c, z, 2 * pair, 0]
                for a, x in [(0, 1), (0, 2), (0, 3), (1, 0), (1, 1), (1, 2), (1, 3)]:
                    lines += norms[c, z, 2 * pair + a, x]
                q = (c * 8 + z * 2 + pair) * 128
                sq[:, q : q + 128] = lines[0:1]
                sq[:, half + q : half + q + 128] = lines[1:2]

    def weights_copy(j, slot):
        return pltpu.make_async_copy(
            upper.at[:, pl.ds(pl.multiple_of(1024 + slot * 512, 512), 512)],
            weights_out.at[:, pl.ds(pl.multiple_of(j * 512, 512), 512)],
            w_sem.at[slot],
        )

    def point_chunk(j, _):
        slot = lax.rem(j, 2)

        @pl.when(j >= 2)
        def _():
            weights_copy(j - 2, slot).wait()

        rows = land[j // 4, lax.rem(j // 2, 2), pl.ds(lax.rem(j, 2) * 2, 2)].reshape(512, 1024)
        cols = pl.ds(pl.multiple_of(j * 512, 512), 512)
        close = jnp.exp2(dot_nt(points[...], rows) * (2.0 * scale) - (factor[...] + sq[:, cols]))
        upper[:, pl.ds(pl.multiple_of(1024 + slot * 512, 512), 512)] = close.astype(BF16)
        image[:count, 128:] += close[:, :128] + close[:, 128:256] + close[:, 256:384] + close[:, 384:]
        weights_copy(j, slot).start()
        return 0

    lax.fori_loop(0, 2, point_chunk, 0)
    for part, c, u in zip(there, there_far, there_up):
        u.wait_recv()
        handed[1].append(forward(part, 2, -1))
        c.wait_recv()
        handed[1].append(forward(part, 2, 2))
    receive(late_ring)
    late_ring = around(late, 1)
    own_norms(1)
    lax.fori_loop(2, 4, point_chunk, 0)
    receive(handed[1])
    lax.fori_loop(4, 8, point_chunk, 0)
    factor[...] = 64.0 / jnp.sqrt(jnp.sum(image[:count, 128:], axis=1, keepdims=True))
    receive(late_ring)
    late_up = [send(part, 2, 0, 1) for part in late]
    late_down = [send(part, 2, 0, -1) for part in late]
    late_handed = [forward(part, 2, 0) for part in late]

    def land_chunk(j, _):
        rows = land[j // 8, lax.rem(j // 4, 2), lax.rem(j, 4)].reshape(256, 1024)
        cols = pl.ds(pl.multiple_of(j * 256, 256), 256)
        inner = dot_nt(land[:, core].reshape(half, 1024), rows)
        close = jnp.exp2(inner * (2.0 * scale) - (col_scale[...] + sq[:, cols]))
        kern[:, cols] = close
        image[:, :128] += close[:, :128] + close[:, 128:]
        csum[0, :, cols] += jnp.sum(close.reshape(half // 8, 8, 256), axis=0)
        return 0

    lax.fori_loop(0, 6, land_chunk, 0)
    receive(late_up + late_down)
    late_far = [send(late[0], 2, -1, 1), send(late[1], 2, 1, -1)]
    late_handed += [forward(part, 2, by) for part in late for by in (-1, 1)]
    lax.fori_loop(6, 12, land_chunk, 0)
    receive(late_far)
    late_handed += [forward(part, 2, 2) for part in late]
    lax.fori_loop(12, 16, land_chunk, 0)

    def swap(src, dst, sems, index):
        c = pltpu.make_async_remote_copy(
            src_ref=src, dst_ref=dst, send_sem=sems.at[0, index], recv_sem=sems.at[1, index],
            device_id=partner, device_id_type=MESH,
        )
        c.start()
        return c

    give = swap(csum.at[0], csum.at[1], c_sem, 0)
    col_scale[...] = 1.0 / jnp.sqrt(jnp.sum(image[:, :128], axis=1, keepdims=True))
    weights_copy(6, 0).wait()
    weights_copy(7, 1).wait()
    receive(late_handed)
    for c in sent + forwarded:
        c.wait_send()
    give.wait_recv()
    row_scale[...] = 1.0 / jnp.sqrt(jnp.sum(csum[0] + csum[1], axis=0, keepdims=True))
    give.wait_send()

    def low_piece(t, s, c):
        return land[s, c, pl.ds(2 * t, 2)].reshape(512, 1024)

    def up_piece(t, s, c):
        cols = pl.ds(pl.multiple_of(s * 2048 + c * 1024, 1024), 1024)
        return upper[pl.ds(pl.multiple_of(t * 512, 512), 512), cols]

    def half_product(piece, t, slot, c):
        rows = jnp.concatenate([piece(t, 0, c), piece(t, 1, c)], axis=1)
        return jnp.dot(rows, xs[slot, :, c].reshape(half, 256), preferred_element_type=F32)

    def scaled(r, b):
        cols = pl.ds(b * 1024, 1024)
        return (kern[r, cols] * col_scale[r, :] * row_scale[:, cols]).astype(BF16)

    def first_low(t, _):
        r = pl.ds(pl.multiple_of(t * 512, 512), 512)
        pieces = []
        for b in range(4):
            piece = scaled(r, b)
            land[b // 2, b % 2, pl.ds(2 * t, 2)] = piece.reshape(2, 4, 4, 16, 1024)
            pieces.append(piece)
        rows = jnp.concatenate(pieces, axis=1)
        image[r, :] = jnp.dot(rows, xs[0].reshape(2 * half, 256), preferred_element_type=F32)
        return 0

    def first_up(t, _):
        r = pl.ds(pl.multiple_of(1024 + t * 512, 512), 512)
        u = pl.ds(pl.multiple_of(t * 512, 512), 512)
        for b in range(4):
            upper[u, pl.ds(b * 1024, 1024)] = scaled(r, b)
        image[r, :] = jnp.dot(upper[u, :], xs[0].reshape(2 * half, 256), preferred_element_type=F32)
        return 0

    eye = lax.broadcasted_iota(jnp.int32, (256, 256), 0) == lax.broadcasted_iota(jnp.int32, (256, 256), 1)
    pending, gives = [], []
    for step in range(ITERS):
        last = step == ITERS - 1
        if step == 0:
            lax.fori_loop(0, 2, first_low, 0)
            lax.fori_loop(0, 2, first_up, 0)
        else:
            def product(piece, base, c, add):
                def tile(t, _):
                    r = pl.ds(pl.multiple_of(base + t * 512, 512), 512)
                    out = half_product(piece, t, step, c)
                    image[r, :] = image[r, :] + out if add else out
                    return 0

                lax.fori_loop(0, 2, tile, 0)

            product(low_piece, 0, core, False)
            product(up_piece, 1024, core, False)
            receive(gives)
            product(up_piece, 1024, 1 - core, True)
            if last:
                weights_in = pltpu.make_async_copy(weights_out, upper, w_sem.at[0])
                weights_in.start()
            product(low_piece, 0, 1 - core, True)
        hi, lo = split(image[...])
        gram = dot_tn(hi, jnp.concatenate([hi, lo], axis=1))
        cross = gram[:, 256:]
        grams[step, 0] = gram[:, :256] + cross + cross.T
        give = swap(grams.at[step, 0], grams.at[step, 1], g_sem, step)
        aug[:, 256:] = jnp.where(eye, 1.0, 0.0)
        give.wait_recv()
        aug[:, :256] = grams[step, 0] + grams[step, 1]
        pending.append(give)
        cholesky_inverse(aug, lower_t, inverse)
        ihi, ilo = split(inverse[...])
        stacked = jnp.concatenate([ihi, ilo, ihi], axis=1)
        if last:
            inverse_lam = 1.0 / jnp.sum(jnp.where(eye, lower_t[...], 0.0), axis=0, keepdims=True)
        gives = []
        target = 0 if last else step + 1
        for t in range(2):
            r = pl.ds(t * 1024, 1024)
            hi, lo = split(image[r, :])
            ortho = dot_nt(jnp.concatenate([hi, hi, lo], axis=1), stacked)
            if last:
                image[r, :] = ortho
                ortho = ortho * col_scale[r, :] * inverse_lam
            xs[target, t, core] = ortho.astype(BF16).reshape(4, 4, 4, 16, 256)
            part = xs.at[target, t, core]
            gives.append(swap(part, part, s_sem if last else x_sem, t))
        pending += gives

    index = at["z"] * 16 + at["y"] * 4 + at["x"]
    for s in range(2):
        rows = pl.ds(pl.multiple_of(s * 1024 + index * 16, 16), 16)
        own_out[16 * s : 16 * s + 16, :] = image[rows, :]
    weights_in.wait()
    for t in range(2):
        image[t * 512 : t * 512 + 512, :] = half_product(up_piece, t, 0, core)
    receive(gives)
    copies = []
    for t in range(2):
        r = pl.ds(t * 512, 512)
        image[r, :] = (image[r, :] + half_product(up_piece, t, 0, 1 - core)) * factor[r, :]
        copies.append(pltpu.make_async_copy(image.at[r, :], coords_out.at[r, :], o_sem.at[t]))
        copies[-1].start()
    for c in pending:
        c.wait_send()
    for c in copies:
        c.wait()


def deliver_kernel(own_ref, coords_ref, own_out, coords_out):
    own_out[...] = own_ref[...]
    coords_out[...] = coords_ref[...]


def body(landmarks, initial_basis, points):
    shard, width = landmarks.shape
    rank = initial_basis.shape[1]
    total = shard * 128
    half = total // 2
    count = points.shape[0]
    scale = LOG2E / (SPREAD * width)
    anywhere = pl.BlockSpec(memory_space=pl.ANY)
    vmem = pl.BlockSpec(memory_space=pltpu.VMEM)
    dma = pltpu.SemaphoreType.DMA
    results = (jax.ShapeDtypeStruct((shard, rank), F32), jax.ShapeDtypeStruct((count, rank), F32))

    own, coords, _ = pl.pallas_call(
        functools.partial(nystrom_kernel, scale),
        name="nystrom",
        out_shape=(*results, jax.ShapeDtypeStruct((count, total), BF16)),
        in_specs=[anywhere, anywhere, anywhere],
        out_specs=(vmem, anywhere, anywhere),
        scratch_shapes=[
            pltpu.VMEM((2, 2, 4, 4, 4, shard // 2, width), BF16),
            pltpu.VMEM((2, 2, 2, 4, 4, 4, shard // 2, rank), BF16),
            pltpu.VMEM((2, 4, 4, 4, 2, 128), F32),
            pltpu.VMEM((half, total), F32),
            pltpu.VMEM((count, total), BF16),
            pltpu.VMEM((half, rank), F32),
            pltpu.VMEM((1, total), F32),
            pltpu.VMEM((2, 8, total), F32),
            pltpu.VMEM((2, 2, rank, rank), F32),
            pltpu.VMEM((rank, 2 * rank), F32),
            pltpu.VMEM((rank, rank), F32),
            pltpu.VMEM((rank, rank), F32),
            pltpu.VMEM((half, 1), F32),
            pltpu.VMEM((1, total), F32),
            pltpu.VMEM((count, 1), F32),
            dma((5,)), dma((81,)), dma((81,)), dma((36,)), dma((36,)), dma((2,)),
            dma((2, 1)), dma((2, 2)), dma((2, 2)), dma((2, 2)), dma((2,)),
        ],
        compiler_params=pltpu.CompilerParams(
            collective_id=0, has_side_effects=True, vmem_limit_bytes=VMEM_LIMIT
        ),
    )(landmarks, initial_basis, points)
    return pl.pallas_call(
        deliver_kernel,
        name="deliver",
        out_shape=results,
        in_specs=[vmem, vmem],
        out_specs=(vmem, vmem),
    )(own, coords)


def solution(mesh):
    in_specs = (P(("grp", "row"), None), P(("grp", "row"), None), P(("grp", "row"), None))
    out_specs = (P(("grp", "row"), None), P(("grp", "row"), None))
    return jax.shard_map(body, mesh=mesh, in_specs=in_specs, out_specs=out_specs, check_vma=False)
```

time: 127 us -> 110 us (0.87)
  Pallas kernels: 122 us -> 109 us
  local copies, waits for them, and re-layouts: 3.64 us -> 0 us
    pallas_call x1, Pallas kernels: 122 us -> 107 us  [body(): pl.pallas_call(functools.partial(nystrom_kernel, scale), name='nystrom',...]
    unnamed x2 -> x0, local copies, waits for them, and re-layouts: 3.64 us -> none
    pallas_call x0 -> x1, Pallas kernels: none -> 2.29 us  [body(): pl.pallas_call(deliver_kernel, name='deliver', out_shape=results, in_spec...]
where the time goes in v3:
time: 110 us; the launch traced here: 109 us
  Pallas kernels  109 us (99%)
    pallas_call x1, Pallas kernels, body(): pl.pallas_call(functools.partial(nystrom_kernel, scale), name='nystrom',...  107 us
    pallas_call x1, Pallas kernels, body(): pl.pallas_call(deliver_kernel, name='deliver', out_shape=results, in_spec...  2.29 us

profile of v3, /device:TPU:1, one launch (start us, length us, event | category | flops | bytes accessed | tf_op | source)
XLA Modules:
  0.0 109.5 jit_solution(5008440145324308142)
XLA Ops:
  0.6 106.6 %nystrom.1 = (f32[32,256]{1,0:T(8,128)}, f32[1024,256]{1,0:T(8,128)}, bf16[1024,4096]{1,0:T(8,128)(2,1)}) custom-call(bf16[32,1024]{1,0:T(8,128)(2,1)} %land_in.1, bf16[32,256]{1,0:T(8,128)(2,1)} %basis_in.1, bf16[1024,1024]{1,0:T(8,128)(2,1)} %points_in.1), custom_call_target="tpu_custom_call" | custom-call | tf_op jit(solution)/shard_map/nystrom/pallas_call | solution.py:444
  107.2 2.3 %deliver.1 = (f32[32,256]{1,0:T(8,128)}, f32[1024,256]{1,0:T(8,128)}) custom-call(f32[32,256]{1,0:T(8,128)} %get-tuple-element.4.own_ref, f32[1024,256]{1,0:T(8,128)} %get-tuple-element.5.coords_ref), custom_call_target="tpu_custom_call" | custom-call | tf_op jit(solution)/shard_map/deliver/pallas_call | solution.py:473

commit v4 on v3

--- a/solution.py
+++ b/solution.py
@@ -123,14 +123,6 @@
         pl.semaphore_signal(barrier, inc=1, device_id=peer, device_id_type=MESH)
     for c in first:
         c.wait()
-    offset = lax.rem(at["y"], 2) * 64 + at["x"] * 16
-    spot = lax.broadcasted_iota(jnp.int32, (16, 128), 1) == lax.broadcasted_iota(jnp.int32, (16, 128), 0) + offset
-    lines = []
-    for s in range(2):
-        mine = land[(s, *own)].astype(F32)
-        own_sq = jnp.sum(mine * mine, axis=1, keepdims=True) * scale
-        lines.append(jnp.sum(jnp.where(spot, own_sq, 0.0), axis=0, keepdims=True))
-    norms[own] = jnp.concatenate(lines, axis=0)
     pl.semaphore_wait(barrier, len(peers))
 
     stages = []
@@ -143,12 +135,14 @@
     stages[0].append((norms, (), EVERY, ORDERS[2]))
     late = [(xs, (0, 0), EVERY, ORDERS[0]), (xs, (0, 1), EVERY, ORDERS[1])]
 
-    def block(part, phase, shift):
+    def block(part, phase, shift, line=None):
         buf, lead, cols, order = part
         index = [*lead, core]
         for a in "zyx":
             if a == order[phase]:
                 index.append(lax.rem(at[a] + shift + 4, 4))
+            elif line is not None and a == order[1]:
+                index.append(lax.rem(at[a] + line + 4, 4))
             elif a in order[:phase]:
                 index.append(EVERY)
             else:
@@ -157,9 +151,9 @@
 
     sent, forwarded = [], []
 
-    def send(part, phase, shift, by):
+    def send(part, phase, shift, by, line=None):
         k = len(sent)
-        ref = block(part, phase, shift)
+        ref = block(part, phase, shift, line)
         c = pltpu.make_async_remote_copy(
             src_ref=ref, dst_ref=ref, send_sem=send_sem.at[k], recv_sem=recv_sem.at[k],
             device_id=neighbour(core, at, part[3][phase], by), device_id_type=MESH,
@@ -180,46 +174,74 @@
         return c
 
     def around(parts, phase):
-        return [send(part, phase, 0, by) for by in (2, 1, -1) for part in parts]
+        return {-by: [send(part, phase, 0, by) for part in parts] for by in (2, 1, -1)}
 
     def receive(copies):
         for c in copies:
             c.wait_recv()
 
-    ring = [around(parts, 0) for parts in stages]
+    def receive_ring(copies):
+        for by in (1, -1, -2):
+            receive(copies[by])
+
+    here, there = stages
+    lines_of = ((0, None), (1, 1), (-1, -1), (2, -2))
+    handed = [[], []]
+    ring = [around(parts, 0) for parts in (stages[0][:3], stages[1])]
+    offset = lax.rem(at["y"], 2) * 64 + at["x"] * 16
+    spot = lax.broadcasted_iota(jnp.int32, (16, 128), 1) == lax.broadcasted_iota(jnp.int32, (16, 128), 0) + offset
+    lines = []
+    for s in range(2):
+        mine = land[(s, *own)].astype(F32)
+        own_sq = jnp.sum(mine * mine, axis=1, keepdims=True) * scale
+        lines.append(jnp.sum(jnp.where(spot, own_sq, 0.0), axis=0, keepdims=True))
+    norms[own] = jnp.concatenate(lines, axis=0)
+    image[...] = jnp.zeros_like(image)
+    csum[0] = jnp.zeros(csum.shape[1:], F32)
+    for by, copies in around(here[3:], 0).items():
+        ring[0][by] += copies
     points_copy.wait()
     wide = points[...].astype(F32)
     factor[...] = jnp.sum(wide * wide, axis=1, keepdims=True) * scale
-    image[...] = jnp.zeros_like(image)
-    csum[0] = jnp.zeros(csum.shape[1:], F32)
-    for s, parts in enumerate(stages):
-        receive(ring[s])
-        ring[s] = around(parts, 1)
-    here, there = stages
-    handed = [[], []]
-    receive(ring[0])
-    here_up = [send(part, 2, 0, 1) for part in here]
-    here_down = [send(part, 2, 0, -1) for part in here]
+    here_up, here_down, there_down = [], [], []
+    receive_ring(ring[0])
+    ring[0] = around(here, 1)
+    here_up.append([send(part, 2, 0, 1, 0) for part in here])
+    here_down.append([send(part, 2, 0, -1, 0) for part in here])
+    receive_ring(ring[1])
+    ring[1] = around(there, 1)
+    there_down.append([send(part, 2, 0, -1, 0) for part in there])
+    for line, source in lines_of[1:]:
+        receive(ring[0][source])
+        here_up.append([send(part, 2, 0, 1, line) for part in here])
+        here_down.append([send(part, 2, 0, -1, line) for part in here])
     handed[0] += [forward(part, 2, 0) for part in here]
-    receive(ring[1])
-    there_down = [send(part, 2, 0, -1) for part in there]
+    here_far = []
+
+    def relay_up(n):
+        receive(here_up[n])
+        here_far.append([send(part, 2, -1, 1, lines_of[n][0]) for part in here])
+
+    relay_up(0)
+    for line, source in lines_of[1:]:
+        receive(ring[1][source])
+        there_down.append([send(part, 2, 0, -1, line) for part in there])
     handed[1] += [forward(part, 2, 0) for part in there]
-    here_far = []
-    for part, c in zip(here, here_up):
-        c.wait_recv()
-        here_far.append(send(part, 2, -1, 1))
+    for n in (1, 2, 3):
+        relay_up(n)
     there_up = [send(part, 2, 0, 1) for part in there]
     handed[0] += [forward(part, 2, -1) for part in here]
-    receive(here_down)
+    for copies in here_down:
+        receive(copies)
     handed[0] += [forward(part, 2, 1) for part in here]
     there_far = []
-    for part, c in zip(there, there_down):
-        c.wait_recv()
-        there_far.append(send(part, 2, 1, -1))
+    for n in range(4):
+        receive(there_down[n])
+        there_far.append([send(part, 2, 1, -1, lines_of[n][0]) for part in there])
     handed[1] += [forward(part, 2, 1) for part in there]
-    for part, c in zip(here, here_far):
-        c.wait_recv()
-        handed[0].append(forward(part, 2, 2))
+    for copies in here_far:
+        receive(copies)
+    handed[0] += [forward(part, 2, 2) for part in here]
     late_ring = around(late, 0)
 
     def own_norms(s):
@@ -227,17 +249,17 @@
         rows = pl.ds(s * (half // 2), half // 2)
         col_scale[rows, :] = jnp.sum(wide * wide, axis=1, keepdims=True) * scale
 
-    own_norms(0)
-    receive(handed[0])
-    for c in range(2):
+    def norms_line(c):
         for z in range(4):
             for pair in range(2):
                 lines = norms[c, z, 2 * pair, 0]
                 for a, x in [(0, 1), (0, 2), (0, 3), (1, 0), (1, 1), (1, 2), (1, 3)]:
                     lines += norms[c, z, 2 * pair + a, x]
-                q = (c * 8 + z * 2 + pair) * 128
-                sq[:, q : q + 128] = lines[0:1]
-                sq[:, half + q : half + q + 128] = lines[1:2]
+                q = pl.multiple_of((c * 8 + z * 2 + pair) * 128, 128)
+                sq[:, pl.ds(q, 128)] = lines[0:1]
+                sq[:, pl.ds(half + q, 128)] = lines[1:2]
+
+    norms_line(core)
 
     def weights_copy(j, slot):
         return pltpu.make_async_copy(
@@ -246,14 +268,16 @@
             w_sem.at[slot],
         )
 
-    def point_chunk(j, _):
-        slot = lax.rem(j, 2)
-
-        @pl.when(j >= 2)
+    def point_chunk(k, _):
+        slot = lax.rem(k, 2)
+
+        @pl.when(k >= 2)
         def _():
-            weights_copy(j - 2, slot).wait()
-
-        rows = land[j // 4, lax.rem(j // 2, 2), pl.ds(lax.rem(j, 2) * 2, 2)].reshape(512, 1024)
+            weights_copy(k - 2, slot).wait()
+
+        s, c = k // 4, lax.rem(lax.rem(k // 2, 2) + core, 2)
+        j = s * 4 + c * 2 + slot
+        rows = land[s, c, pl.ds(slot * 2, 2)].reshape(512, 1024)
         cols = pl.ds(pl.multiple_of(j * 512, 512), 512)
         close = jnp.exp2(dot_nt(points[...], rows) * (2.0 * scale) - (factor[...] + sq[:, cols]))
         upper[:, pl.ds(pl.multiple_of(1024 + slot * 512, 512), 512)] = close.astype(BF16)
@@ -262,19 +286,22 @@
         return 0
 
     lax.fori_loop(0, 2, point_chunk, 0)
-    for part, c, u in zip(there, there_far, there_up):
-        u.wait_recv()
-        handed[1].append(forward(part, 2, -1))
-        c.wait_recv()
-        handed[1].append(forward(part, 2, 2))
-    receive(late_ring)
+    receive(there_up)
+    handed[1] += [forward(part, 2, -1) for part in there]
+    for copies in there_far:
+        receive(copies)
+    handed[1] += [forward(part, 2, 2) for part in there]
+    receive_ring(late_ring)
     late_ring = around(late, 1)
+    receive(handed[0])
+    norms_line(1 - core)
+    lax.fori_loop(2, 4, point_chunk, 0)
+    own_norms(0)
     own_norms(1)
-    lax.fori_loop(2, 4, point_chunk, 0)
     receive(handed[1])
     lax.fori_loop(4, 8, point_chunk, 0)
     factor[...] = 64.0 / jnp.sqrt(jnp.sum(image[:count, 128:], axis=1, keepdims=True))
-    receive(late_ring)
+    receive_ring(late_ring)
     late_up = [send(part, 2, 0, 1) for part in late]
     late_down = [send(part, 2, 0, -1) for part in late]
     late_handed = [forward(part, 2, 0) for part in late]
@@ -463,7 +490,7 @@
             pltpu.VMEM((half, 1), F32),
             pltpu.VMEM((1, total), F32),
             pltpu.VMEM((count, 1), F32),
-            dma((5,)), dma((81,)), dma((81,)), dma((36,)), dma((36,)), dma((2,)),
+            dma((5,)), dma((135,)), dma((135,)), dma((36,)), dma((36,)), dma((2,)),
             dma((2, 1)), dma((2, 2)), dma((2, 2)), dma((2, 2)), dma((2,)),
         ],
         compiler_params=pltpu.CompilerParams(

time: 110 us -> 110 us (level)
  no operation moved by 1% of the time
where the time goes in v4:
time: 110 us; the launch traced here: 109 us
  Pallas kernels  109 us (99%)
    pallas_call x1, Pallas kernels, body(): pl.pallas_call(functools.partial(nystrom_kernel, scale), name='nystrom',...  107 us
    pallas_call x1, Pallas kernels, body(): pl.pallas_call(deliver_kernel, name='deliver', out_shape=results, in_spec...  2.29 us

profile of v4, /device:TPU:1, one launch (start us, length us, event | category | flops | bytes accessed | tf_op | source)
XLA Modules:
  0.0 109.4 jit_solution(7526145587331809906)
XLA Ops:
  0.6 106.5 %nystrom.1 = (f32[32,256]{1,0:T(8,128)}, f32[1024,256]{1,0:T(8,128)}, bf16[1024,4096]{1,0:T(8,128)(2,1)}) custom-call(bf16[32,1024]{1,0:T(8,128)(2,1)} %land_in.1, bf16[32,256]{1,0:T(8,128)(2,1)} %basis_in.1, bf16[1024,1024]{1,0:T(8,128)(2,1)} %points_in.1), custom_call_target="tpu_custom_call" | custom-call | tf_op jit(solution)/shard_map/nystrom/pallas_call | solution.py:471
  107.1 2.3 %deliver.1 = (f32[32,256]{1,0:T(8,128)}, f32[1024,256]{1,0:T(8,128)}) custom-call(f32[32,256]{1,0:T(8,128)} %get-tuple-element.4.own_ref, f32[1024,256]{1,0:T(8,128)} %get-tuple-element.5.coords_ref), custom_call_target="tpu_custom_call" | custom-call | tf_op jit(solution)/shard_map/deliver/pallas_call | solution.py:500

commit v5 on v4

--- a/solution.py
+++ b/solution.py
@@ -244,11 +244,6 @@
     handed[0] += [forward(part, 2, 2) for part in here]
     late_ring = around(late, 0)
 
-    def own_norms(s):
-        wide = land[s, core].reshape(half // 2, 1024).astype(F32)
-        rows = pl.ds(s * (half // 2), half // 2)
-        col_scale[rows, :] = jnp.sum(wide * wide, axis=1, keepdims=True) * scale
-
     def norms_line(c):
         for z in range(4):
             for pair in range(2):
@@ -285,7 +280,13 @@
         weights_copy(j, slot).start()
         return 0
 
-    lax.fori_loop(0, 2, point_chunk, 0)
+    def early_chunk(k, _):
+        wide = land[k // 2, core, pl.ds(lax.rem(k, 2) * 2, 2)].reshape(512, 1024).astype(F32)
+        rows = pl.ds(pl.multiple_of(k * 512, 512), 512)
+        col_scale[rows, :] = jnp.sum(wide * wide, axis=1, keepdims=True) * scale
+        return point_chunk(k, 0)
+
+    lax.fori_loop(0, 2, early_chunk, 0)
     receive(there_up)
     handed[1] += [forward(part, 2, -1) for part in there]
     for copies in there_far:
@@ -295,9 +296,7 @@
     late_ring = around(late, 1)
     receive(handed[0])
     norms_line(1 - core)
-    lax.fori_loop(2, 4, point_chunk, 0)
-    own_norms(0)
-    own_norms(1)
+    lax.fori_loop(2, 4, early_chunk, 0)
     receive(handed[1])
     lax.fori_loop(4, 8, point_chunk, 0)
     factor[...] = 64.0 / jnp.sqrt(jnp.sum(image[:count, 128:], axis=1, keepdims=True))
@@ -316,14 +315,13 @@
         csum[0, :, cols] += jnp.sum(close.reshape(half // 8, 8, 256), axis=0)
         return 0
 
-    lax.fori_loop(0, 6, land_chunk, 0)
+    lax.fori_loop(0, 8, land_chunk, 0)
     receive(late_up + late_down)
     late_far = [send(late[0], 2, -1, 1), send(late[1], 2, 1, -1)]
     late_handed += [forward(part, 2, by) for part in late for by in (-1, 1)]
-    lax.fori_loop(6, 12, land_chunk, 0)
+    lax.fori_loop(8, 16, land_chunk, 0)
     receive(late_far)
     late_handed += [forward(part, 2, 2) for part in late]
-    lax.fori_loop(12, 16, land_chunk, 0)
 
     def swap(src, dst, sems, index):
         c = pltpu.make_async_remote_copy(
@@ -344,15 +342,14 @@
     row_scale[...] = 1.0 / jnp.sqrt(jnp.sum(csum[0] + csum[1], axis=0, keepdims=True))
     give.wait_send()
 
-    def low_piece(t, s, c):
-        return land[s, c, pl.ds(2 * t, 2)].reshape(512, 1024)
-
-    def up_piece(t, s, c):
-        cols = pl.ds(pl.multiple_of(s * 2048 + c * 1024, 1024), 1024)
-        return upper[pl.ds(pl.multiple_of(t * 512, 512), 512), cols]
-
-    def half_product(piece, t, slot, c):
-        rows = jnp.concatenate([piece(t, 0, c), piece(t, 1, c)], axis=1)
+    def low_piece(s, c):
+        return land[s, c].reshape(1024, 1024)
+
+    def up_piece(s, c):
+        return upper[:, pl.ds(pl.multiple_of(s * 2048 + c * 1024, 1024), 1024)]
+
+    def half_product(piece, slot, c):
+        rows = jnp.concatenate([piece(0, c), piece(1, c)], axis=1)
         return jnp.dot(rows, xs[slot, :, c].reshape(half, 256), preferred_element_type=F32)
 
     def scaled(r, b):
@@ -387,13 +384,9 @@
             lax.fori_loop(0, 2, first_up, 0)
         else:
             def product(piece, base, c, add):
-                def tile(t, _):
-                    r = pl.ds(pl.multiple_of(base + t * 512, 512), 512)
-                    out = half_product(piece, t, step, c)
-                    image[r, :] = image[r, :] + out if add else out
-                    return 0
-
-                lax.fori_loop(0, 2, tile, 0)
+                r = pl.ds(base, 1024)
+                out = half_product(piece, step, c)
+                image[r, :] = image[r, :] + out if add else out
 
             product(low_piece, 0, core, False)
             product(up_piece, 1024, core, False)
@@ -436,15 +429,12 @@
         rows = pl.ds(pl.multiple_of(s * 1024 + index * 16, 16), 16)
         own_out[16 * s : 16 * s + 16, :] = image[rows, :]
     weights_in.wait()
-    for t in range(2):
-        image[t * 512 : t * 512 + 512, :] = half_product(up_piece, t, 0, core)
+    image[:count, :] = half_product(up_piece, 0, core)
     receive(gives)
-    copies = []
-    for t in range(2):
-        r = pl.ds(t * 512, 512)
-        image[r, :] = (image[r, :] + half_product(up_piece, t, 0, 1 - core)) * factor[r, :]
-        copies.append(pltpu.make_async_copy(image.at[r, :], coords_out.at[r, :], o_sem.at[t]))
-        copies[-1].start()
+    r = pl.ds(0, count)
+    image[r, :] = (image[r, :] + half_product(up_piece, 0, 1 - core)) * factor[r, :]
+    copies = [pltpu.make_async_copy(image.at[r, :], coords_out, o_sem.at[0])]
+    copies[0].start()
     for c in pending:
         c.wait_send()
     for c in copies:

time: 110 us -> 111 us (level)
    pallas_call x1, Pallas kernels: 107 us -> 108 us  [body(): pl.pallas_call(functools.partial(nystrom_kernel, scale), name='nystrom',...]
where the time goes in v5:
time: 111 us
  Pallas kernels  110 us (99%)
    pallas_call x1, Pallas kernels, body(): pl.pallas_call(functools.partial(nystrom_kernel, scale), name='nystrom',...  108 us
    pallas_call x1, Pallas kernels, body(): pl.pallas_call(deliver_kernel, name='deliver', out_shape=results, in_spec...  2.29 us

profile of v5, /device:TPU:1, one launch (start us, length us, event | category | flops | bytes accessed | tf_op | source)
XLA Modules:
  0.0 110.8 jit_solution(706766525656531420)
XLA Ops:
  0.6 107.9 %nystrom.1 = (f32[32,256]{1,0:T(8,128)}, f32[1024,256]{1,0:T(8,128)}, bf16[1024,4096]{1,0:T(8,128)(2,1)}) custom-call(bf16[32,1024]{1,0:T(8,128)(2,1)} %land_in.1, bf16[32,256]{1,0:T(8,128)(2,1)} %basis_in.1, bf16[1024,1024]{1,0:T(8,128)(2,1)} %points_in.1), custom_call_target="tpu_custom_call" | custom-call | tf_op jit(solution)/shard_map/nystrom/pallas_call | solution.py:461
  108.5 2.3 %deliver.1 = (f32[32,256]{1,0:T(8,128)}, f32[1024,256]{1,0:T(8,128)}) custom-call(f32[32,256]{1,0:T(8,128)} %get-tuple-element.4.own_ref, f32[1024,256]{1,0:T(8,128)} %get-tuple-element.5.coords_ref), custom_call_target="tpu_custom_call" | custom-call | tf_op jit(solution)/shard_map/deliver/pallas_call | solution.py:490

commit v6 on v4

--- a/solution.py
+++ b/solution.py
@@ -244,11 +244,6 @@
     handed[0] += [forward(part, 2, 2) for part in here]
     late_ring = around(late, 0)
 
-    def own_norms(s):
-        wide = land[s, core].reshape(half // 2, 1024).astype(F32)
-        rows = pl.ds(s * (half // 2), half // 2)
-        col_scale[rows, :] = jnp.sum(wide * wide, axis=1, keepdims=True) * scale
-
     def norms_line(c):
         for z in range(4):
             for pair in range(2):
@@ -285,7 +280,13 @@
         weights_copy(j, slot).start()
         return 0
 
-    lax.fori_loop(0, 2, point_chunk, 0)
+    def early_chunk(k, _):
+        wide = land[k // 2, core, pl.ds(lax.rem(k, 2) * 2, 2)].reshape(512, 1024).astype(F32)
+        rows = pl.ds(pl.multiple_of(k * 512, 512), 512)
+        col_scale[rows, :] = jnp.sum(wide * wide, axis=1, keepdims=True) * scale
+        return point_chunk(k, 0)
+
+    lax.fori_loop(0, 2, early_chunk, 0)
     receive(there_up)
     handed[1] += [forward(part, 2, -1) for part in there]
     for copies in there_far:
@@ -295,9 +296,7 @@
     late_ring = around(late, 1)
     receive(handed[0])
     norms_line(1 - core)
-    lax.fori_loop(2, 4, point_chunk, 0)
-    own_norms(0)
-    own_norms(1)
+    lax.fori_loop(2, 4, early_chunk, 0)
     receive(handed[1])
     lax.fori_loop(4, 8, point_chunk, 0)
     factor[...] = 64.0 / jnp.sqrt(jnp.sum(image[:count, 128:], axis=1, keepdims=True))

time: 110 us -> 109 us (level)
  no operation moved by 1% of the time
where the time goes in v6:
time: 109 us
  Pallas kernels  108 us (99%)
    pallas_call x1, Pallas kernels, body(): pl.pallas_call(functools.partial(nystrom_kernel, scale), name='nystrom',...  106 us
    pallas_call x1, Pallas kernels, body(): pl.pallas_call(deliver_kernel, name='deliver', out_shape=results, in_spec...  2.29 us

profile of v6, /device:TPU:1, one launch (start us, length us, event | category | flops | bytes accessed | tf_op | source)
XLA Modules:
  0.0 109.1 jit_solution(1568762590749760966)
XLA Ops:
  0.6 106.2 %nystrom.1 = (f32[32,256]{1,0:T(8,128)}, f32[1024,256]{1,0:T(8,128)}, bf16[1024,4096]{1,0:T(8,128)(2,1)}) custom-call(bf16[32,1024]{1,0:T(8,128)(2,1)} %land_in.1, bf16[32,256]{1,0:T(8,128)(2,1)} %basis_in.1, bf16[1024,1024]{1,0:T(8,128)(2,1)} %points_in.1), custom_call_target="tpu_custom_call" | custom-call | tf_op jit(solution)/shard_map/nystrom/pallas_call | solution.py:470
  106.8 2.3 %deliver.1 = (f32[32,256]{1,0:T(8,128)}, f32[1024,256]{1,0:T(8,128)}) custom-call(f32[32,256]{1,0:T(8,128)} %get-tuple-element.4.own_ref, f32[1024,256]{1,0:T(8,128)} %get-tuple-element.5.coords_ref), custom_call_target="tpu_custom_call" | custom-call | tf_op jit(solution)/shard_map/deliver/pallas_call | solution.py:499
